TPU v7x, 256 devices: a whole 4x4x8 slice. The times are simulated.
256 devices in a mesh: grp: 8 (over z_lo, x), ty: 8 (over z_hi, core), tx: 4 (over y).
Axes of the slice: x: 4, y: 4, z: 8 (z_hi: 4, z_lo: 2; z = z_hi * 2 + z_lo), core: 2. Of those that a mesh axis runs over, the one named last changes fastest.
Arguments:
- noisy: float32 [4, 2048, 1024], P(None, ('grp', 'ty'), 'tx'), may hold values from -6 to 6
- w_in: float32 [64, 4], replicated, may hold values from -3 to 3
- k_first: bfloat16 [3, 3, 64, 64], replicated, may hold values from -0.25 to 0.25
- w_down: bfloat16 [256, 64], replicated, may hold values from -0.75 to 0.75
- k_coarse: bfloat16 [3, 3, 256, 256], replicated, may hold values from -0.125 to 0.125
- w_up: bfloat16 [64, 256], replicated, may hold values from -0.375 to 0.375
- k_last: bfloat16 [3, 3, 64, 64], replicated, may hold values from -0.25 to 0.25
- w_out: bfloat16 [4, 64], replicated, may hold values from -0.75 to 0.75
- station_cell: int32 [64, 4, 128], P(('grp', 'ty'), 'tx'), may hold values from 0 to 8191
- station_count: int32 [64, 4, 128], P(('grp', 'ty'), 'tx'), may hold values from 0 to 3
- observed: float32 [4, 64, 4, 128], P(None, ('grp', 'ty'), 'tx'), may hold values from -6 to 6
Outputs:
- next_state: float32 [4, 2048, 1024], P(None, ('grp', 'ty'), 'tx')
Inputs may be any that keep to these rules, and one draw needn't show every extreme that they name: `station_count`: a count of 0 marks a station without a valid report; several stations may share a cell.
All inputs are finite; a program needn't handle non-finite values.
Results may differ from a plain program's by a relative error of at most 0.017.
Values may be sent and summed in bfloat16 or wider, within the bound.
A program may use at most 64 MiB of HBM per device.

v0:
```python
import jax
import jax.numpy as jnp
from jax import lax
from jax.sharding import PartitionSpec as P

POOL = 32


def extended(block, sides, width):
    for axis, dim in sides:
        count = lax.axis_size(axis)
        forward = [(i, i + 1) for i in range(count - 1)]
        backward = [(target, source) for source, target in forward]
        low = lax.ppermute(
            lax.slice_in_dim(block, block.shape[dim] - width, None, axis=dim), axis, forward
        )
        high = lax.ppermute(lax.slice_in_dim(block, 0, width, axis=dim), axis, backward)
        block = jnp.concatenate([low, block, high], axis=dim)
    return block


def convolve(padded, kernel):
    rows_here = padded.shape[1] - 2
    cols_here = padded.shape[2] - 2
    total = jnp.zeros((kernel.shape[2], rows_here, cols_here), jnp.float32)
    for row_tap in range(3):
        for col_tap in range(3):
            window = padded[:, row_tap : row_tap + rows_here, col_tap : col_tap + cols_here]
            total = total + jnp.einsum(
                "oc,chw->ohw", kernel[row_tap, col_tap], window, preferred_element_type=jnp.float32
            )
    return total


def fine_block(tensor, kernel):
    padded = extended(tensor, ((("grp", "ty"), 1), ("tx", 2)), 1)
    return (tensor.astype(jnp.float32) + jax.nn.silu(convolve(padded, kernel))).astype(jnp.bfloat16)


def on_device(
    noisy,
    w_in,
    k_first,
    w_down,
    k_coarse,
    w_up,
    k_last,
    w_out,
    station_cell,
    station_count,
    observed,
):
    channels = w_in.shape[0]
    rows_here = noisy.shape[1]
    cols_here = noisy.shape[2]
    coarse_rows_here = rows_here // POOL
    coarse_cols_here = cols_here // POOL
    lifted = jnp.einsum("cv,vhw->chw", w_in, noisy).astype(jnp.bfloat16)
    fine_one = fine_block(lifted, k_first)
    pooled = (
        fine_one.astype(jnp.float32)
        .reshape(channels, coarse_rows_here, POOL, coarse_cols_here, POOL)
        .mean(axis=(2, 4))
        .astype(jnp.bfloat16)
    )
    coarse_in = jnp.einsum(
        "dc,chw->dhw", w_down, pooled, preferred_element_type=jnp.float32
    ).astype(jnp.bfloat16)
    padded = extended(coarse_in, ((("grp", "ty"), 1), ("tx", 2)), 1)
    coarse_conv = convolve(padded, k_coarse)
    coarse_out = (coarse_in.astype(jnp.float32) + jax.nn.silu(coarse_conv)).astype(jnp.bfloat16)
    raised = jnp.einsum("cd,dhw->chw", w_up, coarse_out, preferred_element_type=jnp.float32)
    raised = jnp.broadcast_to(
        raised[:, :, None, :, None], (channels, coarse_rows_here, POOL, coarse_cols_here, POOL)
    ).reshape(channels, rows_here, cols_here)
    fine_two = (fine_one.astype(jnp.float32) + raised).astype(jnp.bfloat16)
    fine_three = fine_block(fine_two, k_last)
    denoised = jnp.einsum("vc,chw->vhw", w_out, fine_three, preferred_element_type=jnp.float32)
    flat_field = denoised.reshape(denoised.shape[0], -1)
    cell_index = station_cell.reshape(-1)
    at_station = flat_field[:, cell_index]
    misfit = station_count.reshape(-1).astype(jnp.float32) * (
        observed.reshape(denoised.shape[0], -1) - at_station
    )
    guide = jnp.zeros_like(flat_field).at[:, cell_index].add(misfit).reshape(denoised.shape)
    return noisy + 0.5 * (denoised - noisy) + 0.25 * guide


def solution(mesh):
    return jax.shard_map(
        on_device,
        mesh=mesh,
        in_specs=(
            P(None, ("grp", "ty"), "tx"),
            P(),
            P(),
            P(),
            P(),
            P(),
            P(),
            P(),
            P(("grp", "ty"), "tx", None),
            P(("grp", "ty"), "tx", None),
            P(None, ("grp", "ty"), "tx", None),
        ),
        out_specs=P(None, ("grp", "ty"), "tx"),
        check_vma=False,
    )
```

profile of v0, /device:TPU:32, one launch (start us, length us, event | category | flops | bytes accessed | tf_op | source)
XLA Modules:
  0.0 127.7 jit_solution(13678261580947417734)
XLA Ops:
  0.0 1.4 %convolution_convert_fusion = bf16[64,32,256]{2,0,1:T(8,128)(2,1)S(1)} fusion(f32[4,32,256]{2,1,0:T(8,128)} %param.11, f32[64,4]{0,1:T(4,128)} %param.12), kind=kOutput, calls=%fused_computation.26 | convolution fusion | flops 4194304 | bytes 1180672 | tf_op jit(solution)/shard_map/cv,vhw->chw/dot_general | solution.py:58
  1.5 1.9 %collective-permute-start = (bf16[64,1,256]{2,0,1:T(8,128)(2,1)S(1)}, bf16[64,1,256]{2,0,1:T(8,128)(2,1)S(1)}, u32[]{:S(2)}, u32[]{:S(2)}) collective-permute-start(bf16[64,1,256]{2,0,1:T(8,128)(2,1)S(1)} %get-tuple-element.15), channel_id=1, source_target_pairs={{0,4},{4,8},{8,12},{12,16},{16,20},{20,24},{24,28},{28,32},{32,36}... | collective-permute-start | bytes 98312 | tf_op jit(solution)/shard_map/ppermute | solution.py:14
  3.4 9.4 %collective-permute-start.1 = (bf16[64,1,256]{2,0,1:T(8,128)(2,1)S(1)}, bf16[64,1,256]{2,0,1:T(8,128)(2,1)S(1)}, u32[]{:S(2)}, u32[]{:S(2)}) collective-permute-start(bf16[64,1,256]{2,0,1:T(8,128)(2,1)S(1)} %get-tuple-element.16), channel_id=1, source_target_pairs={{4,0},{8,4},{12,8},{16,12},{20,16},{24,20},{28,24},{32,28},{36,32}... | collective-permute-start | bytes 98312 | tf_op jit(solution)/shard_map/ppermute | solution.py:17
  12.8 1.1 fusion.108
  14.1 0.3 collective-permute-done.1
  14.4 0.1 pad_maximum_fusion.2
  14.5 1.3 %fusion.199 = (bf16[64,34,1]{2,0,1:T(8,128)(2,1)}, bf16[64,34,1]{2,0,1:T(8,128)(2,1)}) fusion(bf16[64,34,256]{2,0,1:T(8,128)(2,1)S(1)} %pad_maximum_fusion.2), kind=kLoop, calls=%fused_computation.222 | loop fusion | bytes 17408 | tf_op jit(solution)/shard_map/slice | solution.py:17
  15.8 1.4 %copy.46 = bf16[64,34,1]{0,1,2:T(8,128)(2,1)S(1)} copy(bf16[64,34,1]{2,0,1:T(8,128)(2,1)} %get-tuple-element.12) | data formatting | bytes 8704 | tf_op jit(solution)/shard_map/slice | solution.py:15
  17.2 3.5 %collective-permute-start.2 = (bf16[64,34,1]{0,1,2:T(8,128)(2,1)S(1)}, bf16[64,34,1]{0,1,2:T(8,128)(2,1)S(1)}, u32[]{:S(2)}, u32[]{:S(2)}) collective-permute-start(bf16[64,34,1]{0,1,2:T(8,128)(2,1)S(1)} %copy.46), channel_id=1, source_target_pairs={{0,1},{1,2},{2,3},{4,5},{5,6},{6,7},{8,9},{9,10},{10,11},{12,13},{... | collective-permute-start | bytes 13064 | tf_op jit(solution)/shard_map/ppermute | solution.py:14
  20.7 1.4 %copy.48 = bf16[64,34,1]{0,1,2:T(8,128)(2,1)S(1)} copy(bf16[64,34,1]{2,0,1:T(8,128)(2,1)} %get-tuple-element.11) | data formatting | bytes 8704 | tf_op jit(solution)/shard_map/slice | solution.py:17
  22.1 1.3 %collective-permute-start.3 = (bf16[64,34,1]{0,1,2:T(8,128)(2,1)S(1)}, bf16[64,34,1]{0,1,2:T(8,128)(2,1)S(1)}, u32[]{:S(2)}, u32[]{:S(2)}) collective-permute-start(bf16[64,34,1]{0,1,2:T(8,128)(2,1)S(1)} %copy.48), channel_id=1, source_target_pairs={{1,0},{2,1},{3,2},{5,4},{6,5},{7,6},{9,8},{10,9},{11,10},{13,12},{... | collective-permute-start | bytes 13064 | tf_op jit(solution)/shard_map/ppermute | solution.py:17
  23.4 2.5 %fusion.45 = f32[32,256,64]{1,2,0:T(8,128)} fusion(bf16[64,1,256]{2,0,1:T(8,128)(2,1)S(1)} %collective-permute-done.1, bf16[64,32,256]{2,0,1:T(8,128)(2,1)S(1)} %convolution_convert_fusion, bf16[3,3,64,64]{3,2,1,0:T(8,128)(2,1)} %param.13), kind=kOutput, calls=%fused_computation.62 | convolution fusion | flops 69206016 | bytes 3194880 | tf_op jit(solution)/shard_map/oc,chw->ohw/dot_general | solution.py:29
  25.8 2.4 %fusion.55 = f32[32,256,64]{1,2,0:T(8,128)} fusion(bf16[64,32,256]{2,0,1:T(8,128)(2,1)S(1)} %convolution_convert_fusion, bf16[64,1,256]{2,0,1:T(8,128)(2,1)S(1)} %collective-permute-done, bf16[3,3,64,64]{3,2,1,0:T(8,128)(2,1)} %param.13), kind=kOutput, calls=%fused_computation.73 | convolution fusion | flops 69206016 | bytes 3194880 | tf_op jit(solution)/shard_map/oc,chw->ohw/dot_general | solution.py:29
  28.3 1.1 copy.47
  29.4 1.1 copy.49
  30.5 2.5 %pad_maximum_fusion = (bf16[64,34,257]{2,0,1:T(8,128)(2,1)S(1)}, bf16[64,34,257]{2,0,1:T(8,128)(2,1)S(1)}) fusion(bf16[64,34,1]{2,0,1:T(8,128)(2,1)} %copy.49, bf16[64,1,256]{2,0,1:T(8,128)(2,1)S(1)} %collective-permute-done.1, bf16[64,32,256]{2,0,1:T(8,128)(2,1)S(1)} %convolution_convert_fusion, bf16[64,1,256]{2,0,1:T(8,128)(2,1)S(1)} %collective-permute-done, ...), kind=kLoop, calls=%fused_computation.23 | loop fusion | flops 8947712 | bytes 3359744 | tf_op jit(solution)/shard_map/concatenate | solution.py:18
  33.0 0.4 fusion.47
  33.4 0.4 fusion.51
  33.8 0.5 fusion.49
  34.3 0.5 fusion.53
  34.8 0.4 fusion.57
  35.3 0.6 copy-done.2
  35.9 0.8 copy-done.1
  36.7 2.8 %convert_reduce_fusion = (f32[64,256]{1,0:T(8,128)S(1)}, bf16[64,32,256]{2,0,1:T(8,128)(2,1)}) fusion(bf16[64,34,257]{2,0,1:T(8,128)(2,1)S(1)} %get-tuple-element.9, bf16[3,3,64,64]{3,2,1,0:T(8,128)(2,1)S(1)} %copy-done.5, f32[32,256,64]{1,2,0:T(8,128)S(1)} %copy-done.1, f32[32,256,64]{1,2,0:T(8,128)S(1)} %fusion.47, f32[32,256,64]{1,2,0:T(8,128)S(1)} %fusion.49, ...), kind=kOutput, calls=%fused_computation.3 | convolution fusion | flops 76005376 | bytes 20004864 | tf_op jit(solution)/shard_map/oc,chw->ohw/dot_general | solution.py:29
  39.7 2.0 %collective-permute-start.4 = (bf16[256,1,8]{0,2,1:T(8,128)(2,1)S(1)}, bf16[256,1,8]{0,2,1:T(8,128)(2,1)S(1)}, u32[]{:S(2)}, u32[]{:S(2)}) collective-permute-start(bf16[256,1,8]{0,2,1:T(8,128)(2,1)S(1)} %bitcast.257), channel_id=1, source_target_pairs={{0,4},{4,8},{8,12},{12,16},{16,20},{20,24},{24,28},{28,32},{32,36}... | collective-permute-start | bytes 12296 | tf_op jit(solution)/shard_map/ppermute | solution.py:14
  41.8 8.8 %collective-permute-start.5 = (bf16[256,1,8]{0,2,1:T(8,128)(2,1)S(1)}, bf16[256,1,8]{0,2,1:T(8,128)(2,1)S(1)}, u32[]{:S(2)}, u32[]{:S(2)}) collective-permute-start(bf16[256,1,8]{0,2,1:T(8,128)(2,1)S(1)} %bitcast.258), channel_id=1, source_target_pairs={{4,0},{8,4},{12,8},{16,12},{20,16},{24,20},{28,24},{32,28},{36,32}... | collective-permute-start | bytes 12296 | tf_op jit(solution)/shard_map/ppermute | solution.py:17
  50.5 1.1 fusion.69
  51.6 0.2 collective-permute-done.5
  51.8 1.3 %collective-permute-start.7 = (bf16[256,3,1]{0,2,1:T(2,128)(2,1)S(1)}, bf16[256,3,1]{0,2,1:T(2,128)(2,1)S(1)}, u32[]{:S(2)}, u32[]{:S(2)}) collective-permute-start(bf16[256,3,1]{0,2,1:T(2,128)(2,1)S(1)} %get-tuple-element.18), channel_id=1, source_target_pairs={{1,0},{2,1},{3,2},{5,4},{6,5},{7,6},{9,8},{10,9},{11,10},{13,12},{... | collective-permute-start | bytes 4616 | tf_op jit(solution)/shard_map/ppermute | solution.py:17
  53.1 5.2 %collective-permute-start.6 = (bf16[256,3,1]{0,2,1:T(2,128)(2,1)S(1)}, bf16[256,3,1]{0,2,1:T(2,128)(2,1)S(1)}, u32[]{:S(2)}, u32[]{:S(2)}) collective-permute-start(bf16[256,3,1]{0,2,1:T(2,128)(2,1)S(1)} %get-tuple-element.17), channel_id=1, source_target_pairs={{0,1},{1,2},{2,3},{4,5},{5,6},{6,7},{8,9},{9,10},{10,11},{12,13},{... | collective-permute-start | bytes 4616 | tf_op jit(solution)/shard_map/ppermute | solution.py:14
  58.3 1.1 fusion.75
  59.4 1.1 fusion.64
  60.4 1.1 fusion.71
  61.5 1.1 fusion.66
  62.6 1.1 fusion.73
  63.7 1.1 fusion.62
  64.8 1.1 fusion.19
  65.9 1.2 convolution_bitcast_fusion
  67.3 0.3 fusion
  67.5 1.9 %collective-permute-start.8 = (bf16[64,1,256]{2,0,1:T(8,128)(2,1)S(1)}, bf16[64,1,256]{2,0,1:T(8,128)(2,1)S(1)}, u32[]{:S(2)}, u32[]{:S(2)}) collective-permute-start(bf16[64,1,256]{2,0,1:T(8,128)(2,1)S(1)} %get-tuple-element.13), channel_id=1, source_target_pairs={{0,4},{4,8},{8,12},{12,16},{16,20},{20,24},{24,28},{28,32},{32,36}... | collective-permute-start | bytes 98312 | tf_op jit(solution)/shard_map/ppermute | solution.py:14
  69.5 8.8 %collective-permute-start.9 = (bf16[64,1,256]{2,0,1:T(8,128)(2,1)S(1)}, bf16[64,1,256]{2,0,1:T(8,128)(2,1)S(1)}, u32[]{:S(2)}, u32[]{:S(2)}) collective-permute-start(bf16[64,1,256]{2,0,1:T(8,128)(2,1)S(1)} %get-tuple-element.14), channel_id=1, source_target_pairs={{4,0},{8,4},{12,8},{16,12},{20,16},{24,20},{28,24},{32,28},{36,32}... | collective-permute-start | bytes 98312 | tf_op jit(solution)/shard_map/ppermute | solution.py:17
  78.2 2.4 %fusion.98 = f32[32,256,64]{1,2,0:T(8,128)} fusion(bf16[64,32,256]{2,0,1:T(8,128)(2,1)S(1)} %fusion, bf16[3,3,64,64]{3,2,1,0:T(8,128)(2,1)} %param.17), kind=kOutput, calls=%fused_computation.118 | convolution fusion | flops 67108864 | bytes 3162112 | tf_op jit(solution)/shard_map/oc,chw->ohw/dot_general | solution.py:29
  80.7 0.1 pad_maximum_fusion.3
  80.8 0.3 fusion.198
  81.1 0.3 copy.52
  81.4 3.9 %collective-permute-start.10 = (bf16[64,34,1]{0,1,2:T(8,128)(2,1)S(1)}, bf16[64,34,1]{0,1,2:T(8,128)(2,1)S(1)}, u32[]{:S(2)}, u32[]{:S(2)}) collective-permute-start(bf16[64,34,1]{0,1,2:T(8,128)(2,1)S(1)} %copy.52), channel_id=1, source_target_pairs={{0,1},{1,2},{2,3},{4,5},{5,6},{6,7},{8,9},{9,10},{10,11},{12,13},{... | collective-permute-start | bytes 13064 | tf_op jit(solution)/shard_map/ppermute | solution.py:14
  85.4 0.3 copy.54
  85.7 1.5 %collective-permute-start.11 = (bf16[64,34,1]{0,1,2:T(8,128)(2,1)S(1)}, bf16[64,34,1]{0,1,2:T(8,128)(2,1)S(1)}, u32[]{:S(2)}, u32[]{:S(2)}) collective-permute-start(bf16[64,34,1]{0,1,2:T(8,128)(2,1)S(1)} %copy.54), channel_id=1, source_target_pairs={{1,0},{2,1},{3,2},{5,4},{6,5},{7,6},{9,8},{10,9},{11,10},{13,12},{... | collective-permute-start | bytes 13064 | tf_op jit(solution)/shard_map/ppermute | solution.py:17
  87.2 2.5 %fusion.37 = f32[32,256,64]{1,2,0:T(8,128)} fusion(bf16[64,32,256]{2,0,1:T(8,128)(2,1)S(1)} %fusion, bf16[64,1,256]{2,0,1:T(8,128)(2,1)S(1)} %collective-permute-done.8, bf16[3,3,64,64]{3,2,1,0:T(8,128)(2,1)} %param.17), kind=kOutput, calls=%fused_computation.55 | convolution fusion | flops 69206016 | bytes 3194880 | tf_op jit(solution)/shard_map/oc,chw->ohw/dot_general | solution.py:29
  89.6 2.5 %fusion.27 = f32[32,256,64]{1,2,0:T(8,128)} fusion(bf16[64,1,256]{2,0,1:T(8,128)(2,1)S(1)} %collective-permute-done.9, bf16[64,32,256]{2,0,1:T(8,128)(2,1)S(1)} %fusion, bf16[3,3,64,64]{3,2,1,0:T(8,128)(2,1)} %param.17), kind=kOutput, calls=%fused_computation.44 | convolution fusion | flops 69206016 | bytes 3194880 | tf_op jit(solution)/shard_map/oc,chw->ohw/dot_general | solution.py:29
  92.1 0.4 copy.53
  92.5 1.1 copy.55
  93.6 2.3 %pad_maximum_fusion.1 = (bf16[64,34,257]{2,0,1:T(8,128)(2,1)S(1)}, bf16[64,34,257]{2,0,1:T(8,128)(2,1)S(1)}) fusion(bf16[64,34,1]{2,0,1:T(8,128)(2,1)} %copy.55, bf16[64,1,256]{2,0,1:T(8,128)(2,1)S(1)} %collective-permute-done.9, bf16[64,32,256]{2,0,1:T(8,128)(2,1)S(1)} %fusion, bf16[64,1,256]{2,0,1:T(8,128)(2,1)S(1)} %collective-permute-done.8, ...), kind=kLoop, calls=%fused_computation.25 | loop fusion | flops 8947712 | bytes 3359744 | tf_op jit(solution)/shard_map/concatenate | solution.py:18
  96.0 1.8 %fusion.29 = f32[32,256,64]{1,2,0:T(8,128)} fusion(bf16[64,34,257]{2,0,1:T(8,128)(2,1)S(1)} %get-tuple-element.6, bf16[3,3,64,64]{3,2,1,0:T(8,128)(2,1)S(1)} %copy-done.6), kind=kOutput, calls=%fused_computation.46 | convolution fusion | flops 67108864 | bytes 3162112 | tf_op jit(solution)/shard_map/oc,chw->ohw/dot_general | solution.py:29
  97.7 1.7 %fusion.33 = f32[32,256,64]{1,2,0:T(8,128)} fusion(bf16[64,34,257]{2,0,1:T(8,128)(2,1)S(1)} %get-tuple-element.6, bf16[3,3,64,64]{3,2,1,0:T(8,128)(2,1)S(1)} %copy-done.6), kind=kOutput, calls=%fused_computation.50 | convolution fusion | flops 67108864 | bytes 3162112 | tf_op jit(solution)/shard_map/oc,chw->ohw/dot_general | solution.py:29
  99.5 1.9 %fusion.31 = f32[32,256,64]{1,2,0:T(8,128)} fusion(bf16[64,34,257]{2,0,1:T(8,128)(2,1)S(1)} %get-tuple-element.5, bf16[3,3,64,64]{3,2,1,0:T(8,128)(2,1)S(1)} %copy-done.6), kind=kOutput, calls=%fused_computation.48 | convolution fusion | flops 67108864 | bytes 3162112 | tf_op jit(solution)/shard_map/oc,chw->ohw/dot_general | solution.py:29
  101.4 1.8 %fusion.35 = f32[32,256,64]{1,2,0:T(8,128)} fusion(bf16[64,34,257]{2,0,1:T(8,128)(2,1)S(1)} %get-tuple-element.5, bf16[3,3,64,64]{3,2,1,0:T(8,128)(2,1)S(1)} %copy-done.6), kind=kOutput, calls=%fused_computation.52 | convolution fusion | flops 67108864 | bytes 3162112 | tf_op jit(solution)/shard_map/oc,chw->ohw/dot_general | solution.py:29
  103.2 1.7 %fusion.39 = f32[32,256,64]{1,2,0:T(8,128)} fusion(bf16[64,34,257]{2,0,1:T(8,128)(2,1)S(1)} %get-tuple-element.6, bf16[3,3,64,64]{3,2,1,0:T(8,128)(2,1)S(1)} %copy-done.6), kind=kOutput, calls=%fused_computation.57 | convolution fusion | flops 67108864 | bytes 3162112 | tf_op jit(solution)/shard_map/oc,chw->ohw/dot_general | solution.py:29
  105.0 7.5 %fusion.25 = f32[32,256,4]{1,2,0:T(4,128)S(1)} fusion(f32[32,256,64]{1,2,0:T(8,128)} %fusion.27, f32[32,256,64]{1,2,0:T(8,128)} %fusion.29, f32[32,256,64]{1,2,0:T(8,128)} %fusion.31, f32[32,256,64]{1,2,0:T(8,128)} %fusion.98, f32[32,256,64]{1,2,0:T(8,128)} %fusion.33, f32[32,256,64]{1,2,0:T(8,128)} %fusion.35, f32[32,256,64]{1,2,0:T(8,128)} %fusion.39, ...), kind=kOutput, calls=%fused_computation.42 | convolution fusion | flops 79167488 | bytes 19022848 | tf_op jit(solution)/shard_map/vc,chw->vhw/dot_general | solution.py:78
  112.5 2.6 %copy.61 = f32[32,256,4]{2,1,0:T(8,128)} copy(f32[32,256,4]{1,2,0:T(4,128)S(1)} %fusion.25) | data formatting | bytes 262144 | tf_op jit(solution)/shard_map/vc,chw->vhw/dot_general | solution.py:78
  115.2 4.5 %scatter_custom_fusion = f32[4,8192]{0,1:T(8,128)} fusion(s32[128]{0:T(128)S(1)} %fusion.181, f32[]{:T(128)} %constant.4.clone.1, f32[4,1,1,128]{0,3,2,1:T(8,128)S(1)} %copy.57, f32[128]{0:T(128)S(1)} %convert_bitcast_fusion, f32[4,8192]{0,1:T(8,128)} %bitcast.254, s32[1024]{0:T(1024)S(1)} %pad_clamp_fusion), kind=kCustom, calls=%fused_computation.18 | custom fusion | flops 1536 | bytes 332292 | tf_op jit(solution)/shard_map/scatter-add | solution.py:85
  119.7 4.5 %broadcast_multiply_fusion = f32[4,8192]{0,1:T(8,128)} fusion(f32[4,8192]{0,1:T(8,128)} %scatter_custom_fusion), kind=kLoop, calls=%fused_computation.5 | loop fusion | flops 32768 | bytes 262144 | tf_op jit(solution)/shard_map/mul | solution.py:86
  124.1 2.9 %copy.63 = f32[4,8192]{1,0:T(4,128)S(1)} copy(f32[4,8192]{0,1:T(8,128)} %broadcast_multiply_fusion) | data formatting | bytes 262144
  127.0 0.7 bitcast_add_fusion
  (44 shorter events, 0.5 us)
Async XLA Ops:
  0.0 39.6 %copy-start = (bf16[256,64]{0,1:T(8,128)(2,1)S(1)}, bf16[256,64]{0,1:T(8,128)(2,1)}, u32[]{:S(2)}) copy-start(bf16[256,64]{0,1:T(8,128)(2,1)} %param.14) | copy-start | bytes 98308
  0.0 14.0 %copy-start.10 = (s32[1,1,128]{2,1,0:T(1,128)S(1)}, s32[1,1,128]{2,1,0:T(1,128)}, u32[]{:S(2)}) copy-start(s32[1,1,128]{2,1,0:T(1,128)} %param.19) | copy-start | bytes 1540
  0.0 14.0 %copy-start.11 = (s32[1,1,128]{2,1,0:T(1,128)S(1)}, s32[1,1,128]{2,1,0:T(1,128)}, u32[]{:S(2)}) copy-start(s32[1,1,128]{2,1,0:T(1,128)} %param.20) | copy-start | bytes 1540
  0.0 14.0 %copy-start.8 = (f32[4,1,1,128]{3,2,1,0:T(1,128)S(1)}, f32[4,1,1,128]{3,2,1,0:T(1,128)}, u32[]{:S(2)}) copy-start(f32[4,1,1,128]{3,2,1,0:T(1,128)} %param.21) | copy-start | bytes 6148
  1.5 12.6 %collective-permute-start = (bf16[64,1,256]{2,0,1:T(8,128)(2,1)S(1)}, bf16[64,1,256]{2,0,1:T(8,128)(2,1)S(1)}, u32[]{:S(2)}, u32[]{:S(2)}) collective-permute-start(bf16[64,1,256]{2,0,1:T(8,128)(2,1)S(1)} %get-tuple-element.15), channel_id=1, source_target_pairs={{0,4},{4,8},{8,12},{12,16},{16,20},{20,24},{24,28},{28,32},{32,36}... | collective-permute-start | bytes 98312 | tf_op jit(solution)/shard_map/ppermute | solution.py:14
  3.4 11.0 %collective-permute-start.1 = (bf16[64,1,256]{2,0,1:T(8,128)(2,1)S(1)}, bf16[64,1,256]{2,0,1:T(8,128)(2,1)S(1)}, u32[]{:S(2)}, u32[]{:S(2)}) collective-permute-start(bf16[64,1,256]{2,0,1:T(8,128)(2,1)S(1)} %get-tuple-element.16), channel_id=1, source_target_pairs={{4,0},{8,4},{12,8},{16,12},{20,16},{24,20},{28,24},{32,28},{36,32}... | collective-permute-start | bytes 98312 | tf_op jit(solution)/shard_map/ppermute | solution.py:17
  17.2 11.0 %collective-permute-start.2 = (bf16[64,34,1]{0,1,2:T(8,128)(2,1)S(1)}, bf16[64,34,1]{0,1,2:T(8,128)(2,1)S(1)}, u32[]{:S(2)}, u32[]{:S(2)}) collective-permute-start(bf16[64,34,1]{0,1,2:T(8,128)(2,1)S(1)} %copy.46), channel_id=1, source_target_pairs={{0,1},{1,2},{2,3},{4,5},{5,6},{6,7},{8,9},{9,10},{10,11},{12,13},{... | collective-permute-start | bytes 13064 | tf_op jit(solution)/shard_map/ppermute | solution.py:14
  22.1 7.3 %collective-permute-start.3 = (bf16[64,34,1]{0,1,2:T(8,128)(2,1)S(1)}, bf16[64,34,1]{0,1,2:T(8,128)(2,1)S(1)}, u32[]{:S(2)}, u32[]{:S(2)}) collective-permute-start(bf16[64,34,1]{0,1,2:T(8,128)(2,1)S(1)} %copy.48), channel_id=1, source_target_pairs={{1,0},{2,1},{3,2},{5,4},{6,5},{7,6},{9,8},{10,9},{11,10},{13,12},{... | collective-permute-start | bytes 13064 | tf_op jit(solution)/shard_map/ppermute | solution.py:17
  30.5 2.5 %copy-start.5 = (bf16[3,3,64,64]{3,2,1,0:T(8,128)(2,1)S(1)}, bf16[3,3,64,64]{3,2,1,0:T(8,128)(2,1)}, u32[]{:S(2)}) copy-start(bf16[3,3,64,64]{3,2,1,0:T(8,128)(2,1)} %param.13) | copy-start | bytes 221188
  34.3 1.6 %copy-start.2 = (f32[32,256,64]{1,2,0:T(8,128)S(1)}, f32[32,256,64]{1,2,0:T(8,128)}, u32[]{:S(2)}) copy-start(f32[32,256,64]{1,2,0:T(8,128)} %fusion.55) | copy-start | bytes 6291460
  34.8 1.8 %copy-start.1 = (f32[32,256,64]{1,2,0:T(8,128)S(1)}, f32[32,256,64]{1,2,0:T(8,128)}, u32[]{:S(2)}) copy-start(f32[32,256,64]{1,2,0:T(8,128)} %fusion.45) | copy-start | bytes 6291460
  36.7 29.2 %copy-start.7 = (bf16[64,256]{1,0:T(8,128)(2,1)S(1)}, bf16[64,256]{1,0:T(8,128)(2,1)}, u32[]{:S(2)}) copy-start(bf16[64,256]{1,0:T(8,128)(2,1)} %param.16) | copy-start | bytes 98308
  39.4 27.8 %copy-start.3 = (bf16[64,32,256]{2,0,1:T(8,128)(2,1)S(1)}, bf16[64,32,256]{2,0,1:T(8,128)(2,1)}, u32[]{:S(2)}) copy-start(bf16[64,32,256]{2,0,1:T(8,128)(2,1)} %get-tuple-element.20) | copy-start | bytes 3145732
  39.7 11.9 %collective-permute-start.4 = (bf16[256,1,8]{0,2,1:T(8,128)(2,1)S(1)}, bf16[256,1,8]{0,2,1:T(8,128)(2,1)S(1)}, u32[]{:S(2)}, u32[]{:S(2)}) collective-permute-start(bf16[256,1,8]{0,2,1:T(8,128)(2,1)S(1)} %bitcast.257), channel_id=1, source_target_pairs={{0,4},{4,8},{8,12},{12,16},{16,20},{20,24},{24,28},{28,32},{32,36}... | collective-permute-start | bytes 12296 | tf_op jit(solution)/shard_map/ppermute | solution.py:14
  41.8 10.1 %collective-permute-start.5 = (bf16[256,1,8]{0,2,1:T(8,128)(2,1)S(1)}, bf16[256,1,8]{0,2,1:T(8,128)(2,1)S(1)}, u32[]{:S(2)}, u32[]{:S(2)}) collective-permute-start(bf16[256,1,8]{0,2,1:T(8,128)(2,1)S(1)} %bitcast.258), channel_id=1, source_target_pairs={{4,0},{8,4},{12,8},{16,12},{20,16},{24,20},{28,24},{32,28},{36,32}... | collective-permute-start | bytes 12296 | tf_op jit(solution)/shard_map/ppermute | solution.py:17
  51.8 10.8 %collective-permute-start.7 = (bf16[256,3,1]{0,2,1:T(2,128)(2,1)S(1)}, bf16[256,3,1]{0,2,1:T(2,128)(2,1)S(1)}, u32[]{:S(2)}, u32[]{:S(2)}) collective-permute-start(bf16[256,3,1]{0,2,1:T(2,128)(2,1)S(1)} %get-tuple-element.18), channel_id=1, source_target_pairs={{1,0},{2,1},{3,2},{5,4},{6,5},{7,6},{9,8},{10,9},{11,10},{13,12},{... | collective-permute-start | bytes 4616 | tf_op jit(solution)/shard_map/ppermute | solution.py:17
  53.1 7.3 %collective-permute-start.6 = (bf16[256,3,1]{0,2,1:T(2,128)(2,1)S(1)}, bf16[256,3,1]{0,2,1:T(2,128)(2,1)S(1)}, u32[]{:S(2)}, u32[]{:S(2)}) collective-permute-start(bf16[256,3,1]{0,2,1:T(2,128)(2,1)S(1)} %get-tuple-element.17), channel_id=1, source_target_pairs={{0,1},{1,2},{2,3},{4,5},{5,6},{6,7},{8,9},{9,10},{10,11},{12,13},{... | collective-permute-start | bytes 4616 | tf_op jit(solution)/shard_map/ppermute | solution.py:14
  67.5 13.1 %collective-permute-start.8 = (bf16[64,1,256]{2,0,1:T(8,128)(2,1)S(1)}, bf16[64,1,256]{2,0,1:T(8,128)(2,1)S(1)}, u32[]{:S(2)}, u32[]{:S(2)}) collective-permute-start(bf16[64,1,256]{2,0,1:T(8,128)(2,1)S(1)} %get-tuple-element.13), channel_id=1, source_target_pairs={{0,4},{4,8},{8,12},{12,16},{16,20},{20,24},{24,28},{28,32},{32,36}... | collective-permute-start | bytes 98312 | tf_op jit(solution)/shard_map/ppermute | solution.py:14
  69.5 11.2 %collective-permute-start.9 = (bf16[64,1,256]{2,0,1:T(8,128)(2,1)S(1)}, bf16[64,1,256]{2,0,1:T(8,128)(2,1)S(1)}, u32[]{:S(2)}, u32[]{:S(2)}) collective-permute-start(bf16[64,1,256]{2,0,1:T(8,128)(2,1)S(1)} %get-tuple-element.14), channel_id=1, source_target_pairs={{4,0},{8,4},{12,8},{16,12},{20,16},{24,20},{28,24},{32,28},{36,32}... | collective-permute-start | bytes 98312 | tf_op jit(solution)/shard_map/ppermute | solution.py:17
  81.4 10.6 %collective-permute-start.10 = (bf16[64,34,1]{0,1,2:T(8,128)(2,1)S(1)}, bf16[64,34,1]{0,1,2:T(8,128)(2,1)S(1)}, u32[]{:S(2)}, u32[]{:S(2)}) collective-permute-start(bf16[64,34,1]{0,1,2:T(8,128)(2,1)S(1)} %copy.52), channel_id=1, source_target_pairs={{0,1},{1,2},{2,3},{4,5},{5,6},{6,7},{8,9},{9,10},{10,11},{12,13},{... | collective-permute-start | bytes 13064 | tf_op jit(solution)/shard_map/ppermute | solution.py:14
  85.7 6.8 %collective-permute-start.11 = (bf16[64,34,1]{0,1,2:T(8,128)(2,1)S(1)}, bf16[64,34,1]{0,1,2:T(8,128)(2,1)S(1)}, u32[]{:S(2)}, u32[]{:S(2)}) collective-permute-start(bf16[64,34,1]{0,1,2:T(8,128)(2,1)S(1)} %copy.54), channel_id=1, source_target_pairs={{1,0},{2,1},{3,2},{5,4},{6,5},{7,6},{9,8},{10,9},{11,10},{13,12},{... | collective-permute-start | bytes 13064 | tf_op jit(solution)/shard_map/ppermute | solution.py:17
  93.6 2.4 %copy-start.6 = (bf16[3,3,64,64]{3,2,1,0:T(8,128)(2,1)S(1)}, bf16[3,3,64,64]{3,2,1,0:T(8,128)(2,1)}, u32[]{:S(2)}) copy-start(bf16[3,3,64,64]{3,2,1,0:T(8,128)(2,1)} %param.17) | copy-start | bytes 221188
  103.2 1.7 %copy-start.9 = (bf16[4,64]{1,0:T(4,128)(2,1)S(1)}, bf16[4,64]{1,0:T(4,128)(2,1)}, u32[]{:S(2)}) copy-start(bf16[4,64]{1,0:T(4,128)(2,1)} %param.18) | copy-start | bytes 1540
  124.1 2.9 %copy-start.4 = (f32[4,32,256]{2,1,0:T(8,128)S(1)}, f32[4,32,256]{2,1,0:T(8,128)}, u32[]{:S(2)}) copy-start(f32[4,32,256]{2,1,0:T(8,128)} %param.11) | copy-start | bytes 393220
where the time goes:
time: 130 us; the launch traced here: 128 us
  starting transfers between devices  49.4 us (38%)
  matrix products  46.4 us (36%)
  local copies, waits for them, and re-layouts  15.9 us (12%)
  other arithmetic  15.1 us (12%)
    dot_general x25, matrix products, convolve(): jnp.einsum('oc,chw->ohw', kernel[row_tap, col_tap], window, preferred_ele...  36.1 us
    ppermute x6, starting transfers between devices, extended(): lax.ppermute(lax.slice_in_dim(block, 0, width, axis=dim), axis, backward)  30.9 us
    ppermute x6, starting transfers between devices, extended(): lax.ppermute(lax.slice_in_dim(block, block.shape[dim] - width, None, axis...  18.4 us
    dot_general x1, matrix products, on_device(): jnp.einsum('vc,chw->vhw', w_out, fine_three, preferred_element_type=jnp.f...  7.54 us
    concatenate x4, other arithmetic, extended(): block = jnp.concatenate([low, block, high], axis=dim)  5.09 us
    scatter-add x1, other arithmetic, on_device(): jnp.zeros_like(flat_field).at[:, cell_index].add(misfit)  4.51 us
    mul x1, other arithmetic, on_device(): return noisy + 0.5 * (denoised - noisy) + 0.25 * guide  4.46 us
    unnamed x26, local copies, waits for them, and re-layouts  4.44 us
  transfers between devices with their start and end apart: 12, of which 2 were waited for; matrix products, arithmetic and copies ran while one was open for 17% of the time, Pallas kernels for 0%

commit v1 on v0

v1 whole, which is shorter than its diff:
```python
import functools

import jax
import jax.numpy as jnp
from jax import lax
from jax.experimental import pallas as pl
from jax.experimental.pallas import tpu as pltpu
from jax.sharding import PartitionSpec as P

F32 = jnp.float32
BF16 = jnp.bfloat16
MESH = pl.DeviceIdType.MESH
NEAR = tuple((dr, dq) for dr in (-1, 0, 1) for dq in (-1, 0, 1) if (dr, dq) != (0, 0))
WIDE = tuple((dr, dq) for dr in (-2, -1, 0, 1, 2) for dq in (-1, 0, 1))
HB = 32
WB = 256
WE = 384
OWN = 9


def dot(a, b):
    return lax.dot_general(a, b, (((1,), (0,)), ((), ())), preferred_element_type=F32)


def dot_t(a, b):
    return lax.dot_general(a, b, (((1,), (1,)), ((), ())), preferred_element_type=F32)


def split2(x):
    high = x.astype(BF16)
    return high, (x - high.astype(F32)).astype(BF16)


def split3(x):
    high = x.astype(BF16)
    rest = x - high.astype(F32)
    middle = rest.astype(BF16)
    return high, middle, (rest - middle.astype(F32)).astype(BF16)


def kernel(
    n_rows,
    n_cols,
    n_ty,
    noisy_h, w_in_h, kf_h, wd_h, kc_h, wu_h, kl_h, wo_h, cell_h, count_h, obs_h,
    out_h,
    noisy_v, w_in_v, kf_v, wd_v, kc_v, wu_v, kl_v, wo_v, cell_v, count_v, obs_v,
    row_send, col_send, row_recv, col_recv, pool_send, pool_recv,
    ext, taps, taps_h, taps_l, a1, a2, w9, wo8, expand, fine, fine_l, fine_r, acc,
    station_a, station_b, fine_three, coarse, up_b, s_ref, raised_ref, out_v,
    in_sem, out_sem, near_send, near_recv, wide_send, wide_recv,
):
    row = lax.axis_index("grp") * n_ty + lax.axis_index("ty")
    col = lax.axis_index("tx")

    def device(dr, dq):
        r = lax.rem(row + dr + n_rows, n_rows)
        q = lax.rem(col + dq + n_cols, n_cols)
        return (r // n_ty, lax.rem(r, n_ty), q)

    def row_ok(dr):
        return jnp.logical_and(row + dr >= 0, row + dr < n_rows)

    def col_ok(dq):
        return jnp.logical_and(col + dq >= 0, col + dq < n_cols)

    pairs = (
        (noisy_h, noisy_v), (w_in_h, w_in_v), (kf_h, kf_v), (kl_h, kl_v), (wo_h, wo_v), (cell_h, cell_v),
        (count_h, count_v), (obs_h, obs_v), (wd_h, wd_v), (wu_h, wu_v), (kc_h, kc_v),
    )
    loads = [pltpu.make_async_copy(src, dst, in_sem.at[k]) for k, (src, dst) in enumerate(pairs)]
    for load in loads:
        load.start()

    barrier = pltpu.get_barrier_semaphore()
    for dr, dq in NEAR:
        pl.semaphore_signal(barrier, inc=1, device_id=device(dr, dq), device_id_type=MESH)

    loads[0].wait()
    for v in range(4):
        row_send[0, 2 * v : 2 * v + 2, :] = noisy_v[v, 0:2, :]
        row_send[1, 2 * v : 2 * v + 2, :] = noisy_v[v, HB - 2 : HB, :]
    first = jnp.concatenate([noisy_v[v, :, 0:128] for v in range(4)], axis=0)
    last = jnp.concatenate([noisy_v[v, :, 128:256] for v in range(4)], axis=0)
    col_send[0] = first.T[0:8, :]
    col_send[1] = last.T[120:128, :]

    pl.semaphore_wait(barrier, len(NEAR))
    near = []
    for k, (dr, dq) in enumerate(NEAR):
        if dq == 0:
            src = row_send.at[0 if dr < 0 else 1]
            dst = row_recv.at[1 if dr < 0 else 0]
        else:
            src = col_send.at[0 if dq < 0 else 1]
            dst = col_recv.at[1 if dq < 0 else 0, 1 - dr]
        back = NEAR.index((-dr, -dq))
        near.append(
            pltpu.make_async_remote_copy(
                src_ref=src, dst_ref=dst, send_sem=near_send.at[k], recv_sem=near_recv.at[back],
                device_id=device(dr, dq), device_id_type=MESH,
            )
        )
    for copy in near:
        copy.start()

    for load in loads[1:]:
        load.wait()
    w_tiled = dot_hi(w_in_v[...])
    lane = lax.broadcasted_iota(jnp.int32, (64, 128), 1)
    zero64 = jnp.zeros((64, 64), BF16)
    kf9 = jnp.concatenate([kf_v[p, q] for p in range(3) for q in range(3)], axis=1)
    for r in range(4):
        placed = []
        for p in range(3):
            for q in range(3):
                at = 12 * (r + p) + 4 * q
                placed.append(jnp.where(jnp.logical_and(lane >= at, lane < at + 4), w_tiled, 0.0))
        placed = jnp.concatenate(placed, axis=0)
        high, middle, low = split3(placed)
        conv = 0.5 * (dot(kf9, high) + dot(kf9, middle) + dot(kf9, low))
        at = 12 * (r + 1) + 4
        lift = jnp.where(jnp.logical_and(lane >= at, lane < at + 4), w_tiled, 0.0)
        high, low = split2(jnp.concatenate([conv, lift], axis=0))
        a1[r, :, 0:80] = high[:, 0:80]
        a1[r, :, 80:160] = high[:, 0:80]
        a1[r, :, 160:240] = low[:, 0:80]
    half = [[(kl_v[p, q].astype(F32) * 0.5).astype(BF16) for q in range(3)] for p in range(3)]
    for q in range(3):
        upper = jnp.concatenate([half[0][q], half[1][q], half[2][q], zero64], axis=1)
        lower = jnp.concatenate([zero64, half[0][q], half[1][q], half[2][q]], axis=1)
        a2[q] = jnp.concatenate([upper, lower], axis=0)
    w9[...] = jnp.concatenate([half[p][q] for p in range(3) for q in range(3)], axis=1)
    pick = (lax.broadcasted_iota(jnp.int32, (32, 4), 0) // 8 == lax.broadcasted_iota(jnp.int32, (32, 4), 1))
    spread = dot(pick.astype(BF16), wo_v[...])
    spread = jnp.concatenate([spread] * 8, axis=1)
    same = lax.broadcasted_iota(jnp.int32, (32, 512), 0) % 8 == lax.broadcasted_iota(jnp.int32, (32, 512), 1) // 64
    wo8[...] = jnp.where(same, spread, 0.0).astype(BF16)
    cells = lax.broadcasted_iota(jnp.int32, (72, WB), 0)
    pixel = lax.broadcasted_iota(jnp.int32, (72, WB), 1)
    for rho in range(3):
        for q in range(3):
            want = rho * 24 + 7 + (pixel + (32 + q - 1)) // 32
            expand[rho * 3 + q] = (cells == want).astype(F32).astype(BF16)

    cell = cell_v[0]
    count = count_v[0].astype(F32)
    at_row = (lax.broadcasted_iota(jnp.int32, (HB, 128), 0) == cell // WB).astype(F32)
    at_col = (lax.broadcasted_iota(jnp.int32, (WB, 128), 0) == cell % WB).astype(F32).astype(BF16)
    reports = [at_row * (count * obs_v[v, 0]) for v in range(4)] + [at_row * count]
    parts = split3(jnp.concatenate(reports, axis=0))
    sums = dot_t(parts[0], at_col) + dot_t(parts[1], at_col) + dot_t(parts[2], at_col)
    for v in range(4):
        station_a[v] = 0.5 * noisy_v[v] + 0.25 * sums[HB * v : HB * (v + 1)]
    station_b[...] = 0.5 - 0.25 * sums[HB * 4 :]

    for copy in near:
        copy.wait()
    ext[...] = jnp.zeros_like(ext)
    for v in range(4):
        ext[v, OWN : OWN + HB, 0:WB] = noisy_v[v]
        ext[v, OWN - 2 : OWN, 0:WB] = jnp.where(row_ok(-1), row_recv[0, 2 * v : 2 * v + 2, :], 0.0)
        ext[v, OWN + HB : OWN + HB + 2, 0:WB] = jnp.where(row_ok(1), row_recv[1, 2 * v : 2 * v + 2, :], 0.0)
    for k in range(3):
        right = jnp.where(jnp.logical_and(row_ok(k - 1), col_ok(1)), col_recv[1, k], 0.0)
        left = jnp.where(jnp.logical_and(row_ok(k - 1), col_ok(-1)), col_recv[0, k], 0.0)
        side = jnp.concatenate([right, jnp.zeros((112, 128), F32), left], axis=0).T
        for v in range(4):
            if k == 0:
                ext[v, OWN - 2 : OWN, WB:WE] = side[HB * v + HB - 2 : HB * v + HB]
            elif k == 1:
                ext[v, OWN : OWN + HB, WB:WE] = side[HB * v : HB * (v + 1)]
            else:
                ext[v, OWN + HB : OWN + HB + 2, WB:WE] = side[HB * v : HB * v + 2]
    for v in range(4):
        for t in range(3):
            here = ext[v, :, 128 * t : 128 * t + 128]
            before = ext[v, :, 128 * ((t + 2) % 3) : 128 * ((t + 2) % 3) + 128]
            after = ext[v, :, 128 * ((t + 1) % 3) : 128 * ((t + 1) % 3) + 128]
            spot = lax.broadcasted_iota(jnp.int32, here.shape, 1)
            shifted = (
                jnp.where(spot < 1, pltpu.roll(before, 1, 1), pltpu.roll(here, 1, 1)),
                here,
                jnp.where(spot < 127, pltpu.roll(here, 127, 1), pltpu.roll(after, 127, 1)),
            )
            for q in range(3):
                taps[t, pl.ds(4 * q + v, 48, stride=12), :] = shifted[q]
    for t in range(3):
        high, low = split2(taps[t])
        taps_h[:, 128 * t : 128 * t + 128] = high
        taps_l[:, 128 * t : 128 * t + 128] = low

    def window(at, lanes):
        high = taps_h[pl.ds(at, 80), lanes]
        return jnp.concatenate([high, taps_l[pl.ds(at, 80), lanes], high], axis=0)

    def gated(both):
        h = both[0:64]
        return both[64:128] + (h + h * jnp.tanh(h))

    def own_rows(g, pool):
        rhs = window(pl.multiple_of(96 + 48 * g, 16), slice(0, WB))
        for r in range(4):
            value = gated(dot(a1[r], rhs))
            at = pl.multiple_of((4 * g + r + 1) * 64, 64)
            fine[pl.ds(at, 64), 0:WB] = value.astype(BF16)
            pool = pool + value
        return pool

    pool = lax.fori_loop(0, 8, own_rows, jnp.zeros((64, WB), F32))
    into = lax.broadcasted_iota(jnp.int32, (8, WB), 1) // 32 == lax.broadcasted_iota(jnp.int32, (8, WB), 0)
    into = into.astype(F32).astype(BF16)
    high, low = split2(jnp.concatenate([pool, jnp.zeros((64, WB), F32)], axis=0))
    pooled = (dot_t(into, high) + dot_t(into, low)) * (1.0 / 1024.0)
    pool_send[...] = pooled
    wide = []
    for k, (dr, dq) in enumerate(WIDE):
        if (dr, dq) == (0, 0):
            continue
        back = WIDE.index((-dr, -dq))
        wide.append(
            pltpu.make_async_remote_copy(
                src_ref=pool_send, dst_ref=pool_recv.at[back], send_sem=wide_send.at[k],
                recv_sem=wide_recv.at[back], device_id=device(dr, dq), device_id_type=MESH,
            )
        )
    for copy in wide:
        copy.start()
    pool_recv[WIDE.index((0, 0))] = pooled

    side_lane = lax.broadcasted_iota(jnp.int32, (64, 128), 1)
    right_gate = jnp.where(col_ok(1), 1.0, 0.0)
    left_gate = jnp.where(col_ok(-1), 1.0, 0.0)
    side_gate = jnp.where(side_lane < 64, right_gate, left_gate)

    def side_rows(g, carry):
        rhs = jnp.concatenate(
            [
                window(pl.multiple_of(96 + 96 * g, 16), slice(WB, WE)),
                window(pl.multiple_of(144 + 96 * g, 16), slice(WB, WE)),
            ],
            axis=1,
        )
        for r in range(4):
            value = gated(dot(a1[r], rhs))
            for k in range(2):
                at = pl.multiple_of((8 * g + 4 * k + r + 1) * 64, 64)
                fine[pl.ds(at, 64), WB:WE] = (value[:, 128 * k : 128 * k + 128] * side_gate).astype(BF16)
        return carry

    lax.fori_loop(0, 4, side_rows, 0)
    for at, r, e, gate in ((48, 3, 0, row_ok(-1)), (480, 0, 33, row_ok(1))):
        gate = jnp.where(gate, 1.0, 0.0)
        value = gated(dot(a1[r], window(at, slice(0, WB)))) * gate
        fine[e * 64 : e * 64 + 64, 0:WB] = value.astype(BF16)
        value = gated(dot(a1[r], window(at, slice(WB, WE)))) * side_gate * gate
        fine[e * 64 : e * 64 + 64, WB:WE] = value.astype(BF16)

    def shift_rows(e, carry):
        at = pl.multiple_of(e * 64, 64)
        tile = [fine[pl.ds(at, 64), 128 * t : 128 * t + 128] for t in range(3)]
        spot = lax.broadcasted_iota(jnp.int32, (64, 128), 1)
        tile = [x.astype(F32) for x in tile]
        up = [pltpu.roll(x, 1, 1) for x in tile]
        down = [pltpu.roll(x, 127, 1) for x in tile]
        fine_l[pl.ds(at, 64), 0:128] = jnp.where(spot < 1, up[2], up[0]).astype(BF16)
        fine_l[pl.ds(at, 64), 128:256] = jnp.where(spot < 1, up[0], up[1]).astype(BF16)
        fine_r[pl.ds(at, 64), 0:128] = jnp.where(spot < 127, down[0], down[1]).astype(BF16)
        fine_r[pl.ds(at, 64), 128:256] = jnp.where(spot < 127, down[1], down[2]).astype(BF16)
        return carry

    lax.fori_loop(0, HB + 2, shift_rows, 0)

    def last_rows(k, carry):
        at = pl.multiple_of(k * 128, 128)
        total = dot(a2[0], fine_l[pl.ds(at, 256), :])
        total += dot(a2[1], fine[pl.ds(at, 256), 0:WB])
        total += dot(a2[2], fine_r[pl.ds(at, 256), :])
        acc[pl.ds(at, 128), :] = total
        return carry

    lax.fori_loop(0, 16, last_rows, 0)

    for copy in wide:
        copy.wait()
    cells = []
    for k, (dr, dq) in enumerate(WIDE):
        cells.append(jnp.where(jnp.logical_and(row_ok(dr), col_ok(dq)), pool_recv[k], 0.0))
    cells = jnp.concatenate(cells, axis=0).astype(BF16)
    entering = dot_t(cells[:, 0:64], wd_v[...])
    coarse[0:8] = jnp.zeros((8, 256), F32)
    coarse[128:136] = jnp.zeros((8, 256), F32)
    coarse[8:128] = entering.astype(BF16).astype(F32)
    total = jnp.zeros((72, 256), F32)
    for p in range(3):
        for q in range(3):
            at = 8 + 24 * p + q - 1
            total += dot_t(coarse[at : at + 72].astype(BF16), kc_v[p, q])
    half_total = 0.5 * total
    leaving = coarse[32:104] + (half_total + half_total * jnp.tanh(half_total))
    blocks = []
    for k, (dr, dq) in enumerate(WIDE[3:12]):
        block = leaving[8 * k : 8 * k + 8]
        blocks.append(jnp.where(jnp.logical_and(row_ok(dr), col_ok(dq)), block, 0.0))
    leaving = jnp.concatenate(blocks, axis=0).astype(BF16)
    high, low = split2(dot_t(wu_v[...], leaving))
    for k in range(9):
        wide_up = dot(high, expand[k])
        up_b[k] = wide_up.astype(BF16)
        if k == 4:
            raised_ref[...] = wide_up + dot(low, expand[k])
    for edge, rhos in enumerate(((0, 1, 1), (1, 1, 1), (1, 1, 2))):
        rhs = jnp.concatenate([up_b[rhos[p] * 3 + q] for p in range(3) for q in range(3)], axis=0)
        s_ref[edge] = dot(w9[...], rhs)

    def finish(i, edge):
        at = i * 64 if isinstance(i, int) else pl.multiple_of(i * 64, 64)
        h = acc[pl.ds(at, 64), :] + s_ref[edge]
        one = fine[pl.ds(at + 64, 64), 0:WB].astype(F32)
        value = one + raised_ref[...] + (h + h * jnp.tanh(h))
        fine_three[pl.ds(at, 64), :] = value.astype(BF16)

    def finish_middle(i, carry):
        finish(i, 1)
        return carry

    finish(0, 0)
    finish(HB - 1, 2)
    lax.fori_loop(1, HB - 1, finish_middle, 0)
    for g in range(4):
        denoised = dot(wo8[...], fine_three[512 * g : 512 * g + 512, :])
        for v in range(4):
            rows = slice(8 * g, 8 * g + 8)
            out_v[v, rows, :] = station_a[v, rows, :] + station_b[rows, :] * denoised[8 * v : 8 * v + 8]
    store = pltpu.make_async_copy(out_v, out_h, out_sem)
    store.start()
    store.wait()


def dot_hi(w_in):
    place = lax.broadcasted_iota(jnp.int32, (4, 128), 1) % 4 == lax.broadcasted_iota(jnp.int32, (4, 128), 0)
    place = place.astype(F32).astype(BF16)
    high, middle, low = split3(w_in)
    return (dot(high, place) + dot(middle, place)) + dot(low, place)


def solution(mesh):
    n_ty = mesh.shape["ty"]
    n_rows = mesh.shape["grp"] * n_ty
    n_cols = mesh.shape["tx"]

    def on_device(noisy, w_in, kf, wd, kc, wu, kl, wo, cell, count, obs):
        obs = obs.reshape(4, 1, 128)
        cell = cell.reshape(1, 1, 128)
        count = count.reshape(1, 1, 128)
        args = (noisy, w_in, kf, wd, kc, wu, kl, wo, cell, count, obs)
        vmem = pltpu.VMEM
        return pl.pallas_call(
            functools.partial(kernel, n_rows, n_cols, n_ty),
            out_shape=jax.ShapeDtypeStruct(noisy.shape, noisy.dtype),
            in_specs=[pl.BlockSpec(memory_space=pl.ANY)] * 11,
            out_specs=pl.BlockSpec(memory_space=pl.ANY),
            scratch_shapes=[vmem(x.shape, x.dtype) for x in args]
            + [
                vmem((2, 8, WB), F32),
                vmem((2, 8, 128), F32),
                vmem((2, 8, WB), F32),
                vmem((2, 3, 8, 128), F32),
                vmem((8, 128), F32),
                vmem((15, 8, 128), F32),
                vmem((4, 48, WE), F32),
                vmem((3, 576, 128), F32),
                vmem((576, WE), BF16),
                vmem((576, WE), BF16),
                vmem((4, 128, 240), BF16),
                vmem((3, 128, 256), BF16),
                vmem((64, 576), BF16),
                vmem((32, 512), BF16),
                vmem((9, 72, WB), BF16),
                vmem((34 * 64, WE), BF16),
                vmem((34 * 64, WB), BF16),
                vmem((34 * 64, WB), BF16),
                vmem((HB * 64, WB), F32),
                vmem((4, HB, WB), F32),
                vmem((HB, WB), F32),
                vmem((HB * 64, WB), BF16),
                vmem((136, 256), F32),
                vmem((9, 64, WB), BF16),
                vmem((3, 64, WB), F32),
                vmem((64, WB), F32),
                vmem((4, HB, WB), F32),
                pltpu.SemaphoreType.DMA((11,)),
                pltpu.SemaphoreType.DMA,
                pltpu.SemaphoreType.DMA((8,)),
                pltpu.SemaphoreType.DMA((8,)),
                pltpu.SemaphoreType.DMA((15,)),
                pltpu.SemaphoreType.DMA((15,)),
            ],
            compiler_params=pltpu.CompilerParams(
                collective_id=0, has_side_effects=True, vmem_limit_bytes=40 * 1024 * 1024
            ),
        )(*args)

    return jax.shard_map(
        on_device,
        mesh=mesh,
        in_specs=(
            P(None, ("grp", "ty"), "tx"),
            P(),
            P(),
            P(),
            P(),
            P(),
            P(),
            P(),
            P(("grp", "ty"), "tx", None),
            P(("grp", "ty"), "tx", None),
            P(None, ("grp", "ty"), "tx", None),
        ),
        out_specs=P(None, ("grp", "ty"), "tx"),
        check_vma=False,
    )
```

time: 130 us -> 39 us (0.30); the launches traced: 128 us -> 38.4 us
  starting transfers between devices: 49.4 us -> 0 us
  matrix products: 46.4 us -> 0 us
  Pallas kernels: 0 us -> 28.6 us
  other arithmetic: 15.1 us -> 0 us
  local copies, waits for them, and re-layouts: 15.9 us -> 9.72 us
    ppermute x12 -> x0, starting transfers between devices: 49.4 us -> none  [the longest x6 30.9 us: extended(): lax.ppermute(lax.slice_in_dim(block, 0, width, axis=dim), axis, backward)]
    dot_general x29 -> x0, matrix products: 46.4 us -> none  [the longest x25 36.1 us: convolve(): jnp.einsum('oc,chw->ohw', kernel[row_tap, col_tap], window, preferred_ele...]
    pallas_call x0 -> x1, Pallas kernels: none -> 28.6 us  [on_device(): pl.pallas_call(functools.partial(kernel, n_rows, n_cols, n_ty), out_shape...]
    unnamed x26 -> x21, local copies, waits for them, and re-layouts: 4.44 us -> 9.72 us
    concatenate x4 -> x0, other arithmetic: 5.09 us -> none  [extended(): block = jnp.concatenate([low, block, high], axis=dim)]
    slice x8 -> x0, local copies, waits for them, and re-layouts: 4.99 us -> none  [the longest x4 3.28 us: extended(): lax.slice_in_dim(block, 0, width, axis=dim)]
    scatter-add x1 -> x0, other arithmetic: 4.51 us -> none  [on_device(): jnp.zeros_like(flat_field).at[:, cell_index].add(misfit)]
    mul x1 -> x0, other arithmetic: 4.46 us -> none  [on_device(): return noisy + 0.5 * (denoised - noisy) + 0.25 * guide]
  transfers between devices with their start and end apart: 12 -> 0, of which waited for: 2 -> 0; matrix products, arithmetic and copies ran while one was open for 17% -> 0% of each run, Pallas kernels for 0% -> 0%
where the time goes in v1:
time: 39 us; the launch traced here: 38.4 us
  Pallas kernels  28.6 us (73%)
  local copies, waits for them, and re-layouts  9.72 us (25%)
    pallas_call x1, Pallas kernels, on_device(): pl.pallas_call(functools.partial(kernel, n_rows, n_cols, n_ty), out_shape...  28.6 us
    unnamed x21, local copies, waits for them, and re-layouts  9.72 us

profile of v1, /device:TPU:32, one launch (start us, length us, event | category | flops | bytes accessed | tf_op | source)
XLA Modules:
  0.0 38.4 jit_solution(16130599661713799722)
XLA Ops:
  0.0 0.8 %copy.12.w_in_h = f32[64,4]{1,0:T(8,128)S(1)} copy(f32[64,4]{0,1:T(4,128)} %param.12) | data formatting | bytes 2048 | tf_op args[1]
  0.8 0.9 %copy.13.wd_h = bf16[256,64]{1,0:T(8,128)(2,1)S(1)} copy(bf16[256,64]{0,1:T(8,128)(2,1)} %param.14) | data formatting | bytes 65536 | tf_op args[3]
  1.6 0.0 copy-start
  1.7 1.3 %copy-done = bf16[3,3,256,256]{3,2,1,0:T(8,128)(2,1)S(1)} copy-done((bf16[3,3,256,256]{3,2,1,0:T(8,128)(2,1)S(1)}, bf16[3,3,256,256]{3,2,1,0:T(8,128)(2,1)}, u32[]{:S(2)}) %copy-start) | copy-done | bytes 1179672
  2.9 0.0 copy-start.1
  2.9 0.9 %copy-done.1 = bf16[3,3,64,64]{3,2,1,0:T(8,128)(2,1)S(1)} copy-done((bf16[3,3,64,64]{3,2,1,0:T(8,128)(2,1)S(1)}, bf16[3,3,64,64]{3,2,1,0:T(8,128)(2,1)}, u32[]{:S(2)}) %copy-start.1) | copy-done | bytes 73752
  3.8 0.0 copy-start.2
  3.8 0.9 %copy-done.2 = bf16[3,3,64,64]{3,2,1,0:T(8,128)(2,1)S(1)} copy-done((bf16[3,3,64,64]{3,2,1,0:T(8,128)(2,1)S(1)}, bf16[3,3,64,64]{3,2,1,0:T(8,128)(2,1)}, u32[]{:S(2)}) %copy-start.2) | copy-done | bytes 73752
  4.7 0.0 copy-start.3
  4.7 0.9 %copy-done.3 = f32[4,32,256]{2,1,0:T(8,128)S(1)} copy-done((f32[4,32,256]{2,1,0:T(8,128)S(1)}, f32[4,32,256]{2,1,0:T(8,128)}, u32[]{:S(2)}) %copy-start.3) | copy-done | bytes 131096
  5.6 0.0 copy-start.4
  5.6 0.8 %copy-done.4 = bf16[64,256]{1,0:T(8,128)(2,1)S(1)} copy-done((bf16[64,256]{1,0:T(8,128)(2,1)S(1)}, bf16[64,256]{1,0:T(8,128)(2,1)}, u32[]{:S(2)}) %copy-start.4) | copy-done | bytes 32792
  6.4 0.0 copy-start.5
  6.4 0.7 %copy-done.5 = f32[4,1,1,128]{3,2,1,0:T(1,128)S(1)} copy-done((f32[4,1,1,128]{3,2,1,0:T(1,128)S(1)}, f32[4,1,1,128]{3,2,1,0:T(1,128)}, u32[]{:S(2)}) %copy-start.5) | copy-done | bytes 2072
  7.1 0.0 copy-start.6
  7.1 0.7 %copy-done.6 = bf16[4,64]{1,0:T(4,128)(2,1)S(1)} copy-done((bf16[4,64]{1,0:T(4,128)(2,1)S(1)}, bf16[4,64]{1,0:T(4,128)(2,1)}, u32[]{:S(2)}) %copy-start.6) | copy-done | bytes 536
  7.8 0.0 copy-start.7
  7.8 0.7 %copy-done.7 = s32[1,1,128]{2,1,0:T(1,128)S(1)} copy-done((s32[1,1,128]{2,1,0:T(1,128)S(1)}, s32[1,1,128]{2,1,0:T(1,128)}, u32[]{:S(2)}) %copy-start.7) | copy-done | bytes 536
  8.4 0.0 copy-start.8
  8.4 0.7 %copy-done.8 = s32[1,1,128]{2,1,0:T(1,128)S(1)} copy-done((s32[1,1,128]{2,1,0:T(1,128)S(1)}, s32[1,1,128]{2,1,0:T(1,128)}, u32[]{:S(2)}) %copy-start.8) | copy-done | bytes 536
  9.1 28.6 %shard_map.109 = f32[4,32,256]{2,1,0:T(8,128)S(1)} custom-call(f32[4,32,256]{2,1,0:T(8,128)S(1)} %copy-done.3, f32[64,4]{1,0:T(8,128)S(1)} %copy.12.w_in_h, bf16[3,3,64,64]{3,2,1,0:T(8,128)(2,1)S(1)} %copy-done.1, bf16[256,64]{1,0:T(8,128)(2,1)S(1)} %copy.13.wd_h, bf16[3,3,256,256]{3,2,1,0:T(8,128)(2,1)S(1)} %copy-done, bf16[64,256]{1,0:T(8,128)(2,1)S(1)} %copy-done.4, ...), custom_call_target="tpu_custom_call" | custom-call | tf_op jit(solution)/shard_map/pallas_call | solution.py:358
  37.7 0.7 %copy.15 = f32[4,32,256]{2,1,0:T(8,128)} copy(f32[4,32,256]{2,1,0:T(8,128)S(1)} %shard_map.109) | data formatting | bytes 262144
Async XLA Ops:
  1.6 1.3 %copy-start = (bf16[3,3,256,256]{3,2,1,0:T(8,128)(2,1)S(1)}, bf16[3,3,256,256]{3,2,1,0:T(8,128)(2,1)}, u32[]{:S(2)}) copy-start(bf16[3,3,256,256]{3,2,1,0:T(8,128)(2,1)} %kc_h.1) | copy-start | bytes 3538948
  2.9 0.9 %copy-start.1 = (bf16[3,3,64,64]{3,2,1,0:T(8,128)(2,1)S(1)}, bf16[3,3,64,64]{3,2,1,0:T(8,128)(2,1)}, u32[]{:S(2)}) copy-start(bf16[3,3,64,64]{3,2,1,0:T(8,128)(2,1)} %kf_h.1) | copy-start | bytes 221188
  3.8 0.9 %copy-start.2 = (bf16[3,3,64,64]{3,2,1,0:T(8,128)(2,1)S(1)}, bf16[3,3,64,64]{3,2,1,0:T(8,128)(2,1)}, u32[]{:S(2)}) copy-start(bf16[3,3,64,64]{3,2,1,0:T(8,128)(2,1)} %kl_h.1) | copy-start | bytes 221188
  4.7 0.9 %copy-start.3 = (f32[4,32,256]{2,1,0:T(8,128)S(1)}, f32[4,32,256]{2,1,0:T(8,128)}, u32[]{:S(2)}) copy-start(f32[4,32,256]{2,1,0:T(8,128)} %noisy_h.1) | copy-start | bytes 393220
  5.6 0.8 %copy-start.4 = (bf16[64,256]{1,0:T(8,128)(2,1)S(1)}, bf16[64,256]{1,0:T(8,128)(2,1)}, u32[]{:S(2)}) copy-start(bf16[64,256]{1,0:T(8,128)(2,1)} %wu_h.1) | copy-start | bytes 98308
  6.4 0.7 %copy-start.5 = (f32[4,1,1,128]{3,2,1,0:T(1,128)S(1)}, f32[4,1,1,128]{3,2,1,0:T(1,128)}, u32[]{:S(2)}) copy-start(f32[4,1,1,128]{3,2,1,0:T(1,128)} %param.21) | copy-start | bytes 6148
  7.1 0.7 %copy-start.6 = (bf16[4,64]{1,0:T(4,128)(2,1)S(1)}, bf16[4,64]{1,0:T(4,128)(2,1)}, u32[]{:S(2)}) copy-start(bf16[4,64]{1,0:T(4,128)(2,1)} %wo_h.1) | copy-start | bytes 1540
  7.8 0.7 %copy-start.7 = (s32[1,1,128]{2,1,0:T(1,128)S(1)}, s32[1,1,128]{2,1,0:T(1,128)}, u32[]{:S(2)}) copy-start(s32[1,1,128]{2,1,0:T(1,128)} %cell_h.1) | copy-start | bytes 1540
  8.4 0.7 %copy-start.8 = (s32[1,1,128]{2,1,0:T(1,128)S(1)}, s32[1,1,128]{2,1,0:T(1,128)}, u32[]{:S(2)}) copy-start(s32[1,1,128]{2,1,0:T(1,128)} %count_h.1) | copy-start | bytes 1540

commit v2 on v1

--- a/solution.py
+++ b/solution.py
@@ -106,7 +106,7 @@
 
     for load in loads[1:]:
         load.wait()
-    w_tiled = dot_hi(w_in_v[...])
+    w_tiled = dot_hi(w_in_v[...].T)
     lane = lax.broadcasted_iota(jnp.int32, (64, 128), 1)
     zero64 = jnp.zeros((64, 64), BF16)
     kf9 = jnp.concatenate([kf_v[p, q] for p in range(3) for q in range(3)], axis=1)
@@ -207,7 +207,7 @@
             pool = pool + value
         return pool
 
-    pool = lax.fori_loop(0, 8, own_rows, jnp.zeros((64, WB), F32))
+    pool = lax.fori_loop(0, 8, own_rows, jnp.zeros((64, WB), F32), unroll=True)
     into = lax.broadcasted_iota(jnp.int32, (8, WB), 1) // 32 == lax.broadcasted_iota(jnp.int32, (8, WB), 0)
     into = into.astype(F32).astype(BF16)
     high, low = split2(jnp.concatenate([pool, jnp.zeros((64, WB), F32)], axis=0))
@@ -248,7 +248,7 @@
                 fine[pl.ds(at, 64), WB:WE] = (value[:, 128 * k : 128 * k + 128] * side_gate).astype(BF16)
         return carry
 
-    lax.fori_loop(0, 4, side_rows, 0)
+    lax.fori_loop(0, 4, side_rows, 0, unroll=True)
     for at, r, e, gate in ((48, 3, 0, row_ok(-1)), (480, 0, 33, row_ok(1))):
         gate = jnp.where(gate, 1.0, 0.0)
         value = gated(dot(a1[r], window(at, slice(0, WB)))) * gate
@@ -269,7 +269,7 @@
         fine_r[pl.ds(at, 64), 128:256] = jnp.where(spot < 127, down[1], down[2]).astype(BF16)
         return carry
 
-    lax.fori_loop(0, HB + 2, shift_rows, 0)
+    lax.fori_loop(0, HB + 2, shift_rows, 0, unroll=True)
 
     def last_rows(k, carry):
         at = pl.multiple_of(k * 128, 128)
@@ -279,7 +279,7 @@
         acc[pl.ds(at, 128), :] = total
         return carry
 
-    lax.fori_loop(0, 16, last_rows, 0)
+    lax.fori_loop(0, 16, last_rows, 0, unroll=True)
 
     for copy in wide:
         copy.wait()
@@ -287,7 +287,7 @@
     for k, (dr, dq) in enumerate(WIDE):
         cells.append(jnp.where(jnp.logical_and(row_ok(dr), col_ok(dq)), pool_recv[k], 0.0))
     cells = jnp.concatenate(cells, axis=0).astype(BF16)
-    entering = dot_t(cells[:, 0:64], wd_v[...])
+    entering = dot(cells[:, 0:64], wd_v[...])
     coarse[0:8] = jnp.zeros((8, 256), F32)
     coarse[128:136] = jnp.zeros((8, 256), F32)
     coarse[8:128] = entering.astype(BF16).astype(F32)
@@ -326,7 +326,7 @@
 
     finish(0, 0)
     finish(HB - 1, 2)
-    lax.fori_loop(1, HB - 1, finish_middle, 0)
+    lax.fori_loop(1, HB - 1, finish_middle, 0, unroll=True)
     for g in range(4):
         denoised = dot(wo8[...], fine_three[512 * g : 512 * g + 512, :])
         for v in range(4):
@@ -350,6 +350,7 @@
     n_cols = mesh.shape["tx"]
 
     def on_device(noisy, w_in, kf, wd, kc, wu, kl, wo, cell, count, obs):
+        w_in, wd = w_in.T, wd.T
         obs = obs.reshape(4, 1, 128)
         cell = cell.reshape(1, 1, 128)
         count = count.reshape(1, 1, 128)
@@ -358,7 +359,7 @@
         return pl.pallas_call(
             functools.partial(kernel, n_rows, n_cols, n_ty),
             out_shape=jax.ShapeDtypeStruct(noisy.shape, noisy.dtype),
-            in_specs=[pl.BlockSpec(memory_space=pl.ANY)] * 11,
+            in_specs=[pl.BlockSpec(memory_space=pltpu.HBM)] * 11,
             out_specs=pl.BlockSpec(memory_space=pl.ANY),
             scratch_shapes=[vmem(x.shape, x.dtype) for x in args]
             + [
@@ -397,7 +398,7 @@
                 pltpu.SemaphoreType.DMA((15,)),
             ],
             compiler_params=pltpu.CompilerParams(
-                collective_id=0, has_side_effects=True, vmem_limit_bytes=40 * 1024 * 1024
+                collective_id=0, has_side_effects=True, vmem_limit_bytes=67043328
             ),
         )(*args)
 

time: 39 us -> 28.1 us (0.72)
  local copies, waits for them, and re-layouts: 9.72 us -> 1.57 us
  Pallas kernels: 28.6 us -> 26.2 us
    unnamed x21 -> x1, local copies, waits for them, and re-layouts: 9.72 us -> 1.57 us
    pallas_call x1, Pallas kernels: 28.6 us -> 26.2 us  [on_device(): pl.pallas_call(functools.partial(kernel, n_rows, n_cols, n_ty), out_shape...]
where the time goes in v2:
time: 28.1 us; the launch traced here: 27.7 us
  Pallas kernels  26.2 us (93%)
  local copies, waits for them, and re-layouts  1.57 us (6%)
    pallas_call x1, Pallas kernels, on_device(): pl.pallas_call(functools.partial(kernel, n_rows, n_cols, n_ty), out_shape...  26.2 us
    unnamed x1, local copies, waits for them, and re-layouts  1.57 us

profile of v2, /device:TPU:32, one launch (start us, length us, event | category | flops | bytes accessed | tf_op | source)
XLA Modules:
  0.0 27.7 jit_solution(12150467999083106156)
XLA Ops:
  0.0 26.2 %shard_map.109 = f32[4,32,256]{2,1,0:T(8,128)} custom-call(f32[4,32,256]{2,1,0:T(8,128)} %noisy_h.1, f32[4,64]{1,0:T(4,128)} %bitcast.4, bf16[3,3,64,64]{3,2,1,0:T(8,128)(2,1)} %kf_h.1, bf16[64,256]{1,0:T(8,128)(2,1)} %bitcast.3, bf16[3,3,256,256]{3,2,1,0:T(8,128)(2,1)} %kc_h.1, bf16[64,256]{1,0:T(8,128)(2,1)} %wu_h.1, bf16[3,3,64,64]{3,2,1,0:T(8,128)(2,1)} %kl_h.1, ...), custom_call_target="tpu_custom_call" | custom-call | tf_op jit(solution)/shard_map/pallas_call | solution.py:359
  26.2 1.6 %copy.13 = f32[4,32,256]{2,1,0:T(8,128)} copy(f32[4,32,256]{2,1,0:T(8,128)} %shard_map.109) | data formatting | bytes 262144

commit v3 on v2

--- a/solution.py
+++ b/solution.py
@@ -73,8 +73,9 @@
         load.start()
 
     barrier = pltpu.get_barrier_semaphore()
-    for dr, dq in NEAR:
-        pl.semaphore_signal(barrier, inc=1, device_id=device(dr, dq), device_id_type=MESH)
+    for dr, dq in WIDE:
+        if (dr, dq) != (0, 0):
+            pl.semaphore_signal(barrier, inc=1, device_id=device(dr, dq), device_id_type=MESH)
 
     loads[0].wait()
     for v in range(4):
@@ -85,7 +86,7 @@
     col_send[0] = first.T[0:8, :]
     col_send[1] = last.T[120:128, :]
 
-    pl.semaphore_wait(barrier, len(NEAR))
+    pl.semaphore_wait(barrier, len(WIDE) - 1)
     near = []
     for k, (dr, dq) in enumerate(NEAR):
         if dq == 0:
@@ -154,41 +155,44 @@
         station_a[v] = 0.5 * noisy_v[v] + 0.25 * sums[HB * v : HB * (v + 1)]
     station_b[...] = 0.5 - 0.25 * sums[HB * 4 :]
 
-    for copy in near:
-        copy.wait()
+    for k, (dr, dq) in enumerate(NEAR):
+        if dr >= 0:
+            near[k].wait_recv()
     ext[...] = jnp.zeros_like(ext)
+
+    def side_columns(k):
+        right = jnp.where(jnp.logical_and(row_ok(k - 1), col_ok(1)), col_recv[1, k], 0.0)
+        left = jnp.where(jnp.logical_and(row_ok(k - 1), col_ok(-1)), col_recv[0, k], 0.0)
+        return jnp.concatenate([right, jnp.zeros((112, 128), F32), left], axis=0).T
+
+    above, beside = side_columns(0), side_columns(1)
     for v in range(4):
         ext[v, OWN : OWN + HB, 0:WB] = noisy_v[v]
         ext[v, OWN - 2 : OWN, 0:WB] = jnp.where(row_ok(-1), row_recv[0, 2 * v : 2 * v + 2, :], 0.0)
-        ext[v, OWN + HB : OWN + HB + 2, 0:WB] = jnp.where(row_ok(1), row_recv[1, 2 * v : 2 * v + 2, :], 0.0)
-    for k in range(3):
-        right = jnp.where(jnp.logical_and(row_ok(k - 1), col_ok(1)), col_recv[1, k], 0.0)
-        left = jnp.where(jnp.logical_and(row_ok(k - 1), col_ok(-1)), col_recv[0, k], 0.0)
-        side = jnp.concatenate([right, jnp.zeros((112, 128), F32), left], axis=0).T
+        ext[v, OWN - 2 : OWN, WB:WE] = above[HB * v + HB - 2 : HB * v + HB]
+        ext[v, OWN : OWN + HB, WB:WE] = beside[HB * v : HB * (v + 1)]
+
+    def make_taps(start, size):
         for v in range(4):
-            if k == 0:
-                ext[v, OWN - 2 : OWN, WB:WE] = side[HB * v + HB - 2 : HB * v + HB]
-            elif k == 1:
-                ext[v, OWN : OWN + HB, WB:WE] = side[HB * v : HB * (v + 1)]
-            else:
-                ext[v, OWN + HB : OWN + HB + 2, WB:WE] = side[HB * v : HB * v + 2]
-    for v in range(4):
+            for t in range(3):
+                here, before, after = (
+                    ext[v, start : start + size, 128 * ((t + d) % 3) : 128 * ((t + d) % 3) + 128] for d in (0, 2, 1)
+                )
+                spot = lax.broadcasted_iota(jnp.int32, here.shape, 1)
+                shifted = (
+                    jnp.where(spot < 1, pltpu.roll(before, 1, 1), pltpu.roll(here, 1, 1)),
+                    here,
+                    jnp.where(spot < 127, pltpu.roll(here, 127, 1), pltpu.roll(after, 127, 1)),
+                )
+                for q in range(3):
+                    taps[t, pl.ds(12 * start + 4 * q + v, size, stride=12), :] = shifted[q]
+        rows = slice(12 * start, 12 * (start + size))
         for t in range(3):
-            here = ext[v, :, 128 * t : 128 * t + 128]
-            before = ext[v, :, 128 * ((t + 2) % 3) : 128 * ((t + 2) % 3) + 128]
-            after = ext[v, :, 128 * ((t + 1) % 3) : 128 * ((t + 1) % 3) + 128]
-            spot = lax.broadcasted_iota(jnp.int32, here.shape, 1)
-            shifted = (
-                jnp.where(spot < 1, pltpu.roll(before, 1, 1), pltpu.roll(here, 1, 1)),
-                here,
-                jnp.where(spot < 127, pltpu.roll(here, 127, 1), pltpu.roll(after, 127, 1)),
-            )
-            for q in range(3):
-                taps[t, pl.ds(4 * q + v, 48, stride=12), :] = shifted[q]
-    for t in range(3):
-        high, low = split2(taps[t])
-        taps_h[:, 128 * t : 128 * t + 128] = high
-        taps_l[:, 128 * t : 128 * t + 128] = low
+            high, low = split2(taps[t, rows])
+            taps_h[rows, 128 * t : 128 * t + 128] = high
+            taps_l[rows, 128 * t : 128 * t + 128] = low
+
+    make_taps(0, 48)
 
     def window(at, lanes):
         high = taps_h[pl.ds(at, 80), lanes]
@@ -198,35 +202,71 @@
         h = both[0:64]
         return both[64:128] + (h + h * jnp.tanh(h))
 
-    def own_rows(g, pool):
-        rhs = window(pl.multiple_of(96 + 48 * g, 16), slice(0, WB))
-        for r in range(4):
-            value = gated(dot(a1[r], rhs))
-            at = pl.multiple_of((4 * g + r + 1) * 64, 64)
-            fine[pl.ds(at, 64), 0:WB] = value.astype(BF16)
-            pool = pool + value
-        return pool
-
-    pool = lax.fori_loop(0, 8, own_rows, jnp.zeros((64, WB), F32), unroll=True)
+    def fine_row(i, rhs, gate=None):
+        value = gated(dot(a1[i % 4], rhs))
+        if gate is not None:
+            value = value * jnp.where(gate, 1.0, 0.0)
+        fine[64 * (i + 1) : 64 * (i + 2), 0:WB] = value.astype(BF16)
+        return value
+
     into = lax.broadcasted_iota(jnp.int32, (8, WB), 1) // 32 == lax.broadcasted_iota(jnp.int32, (8, WB), 0)
     into = into.astype(F32).astype(BF16)
-    high, low = split2(jnp.concatenate([pool, jnp.zeros((64, WB), F32)], axis=0))
-    pooled = (dot_t(into, high) + dot_t(into, low)) * (1.0 / 1024.0)
-    pool_send[...] = pooled
+
+    def sums_of(upper, lower):
+        high, low = split2(jnp.concatenate([upper, lower], axis=0))
+        return (dot_t(into, high) + dot_t(into, low)) * (1.0 / 1024.0)
+
+    middle = jnp.zeros((64, WB), F32)
+    for g in range(8):
+        rhs = window(96 + 48 * g, slice(0, WB))
+        for r in range(4):
+            i = 4 * g + r
+            if i < HB - 1:
+                value = fine_row(i, rhs)
+                if i == 0:
+                    first_row = value
+                else:
+                    middle = middle + value
+    outer_row = fine_row(-1, window(48, slice(0, WB)), row_ok(-1))
+    tile = sums_of(middle + first_row, outer_row)
+    pool_send[0] = tile
     wide = []
-    for k, (dr, dq) in enumerate(WIDE):
-        if (dr, dq) == (0, 0):
-            continue
-        back = WIDE.index((-dr, -dq))
+
+    def send(which, dr, dq, slot):
         wide.append(
             pltpu.make_async_remote_copy(
-                src_ref=pool_send, dst_ref=pool_recv.at[back], send_sem=wide_send.at[k],
-                recv_sem=wide_recv.at[back], device_id=device(dr, dq), device_id_type=MESH,
+                src_ref=pool_send.at[which], dst_ref=pool_recv.at[slot], send_sem=wide_send.at[len(wide)],
+                recv_sem=wide_recv.at[slot], device_id=device(dr, dq), device_id_type=MESH,
             )
         )
-    for copy in wide:
-        copy.start()
-    pool_recv[WIDE.index((0, 0))] = pooled
+        wide[-1].start()
+
+    for dr in (1, 2):
+        for dq in (-1, 0, 1):
+            send(0, dr, dq, WIDE.index((-dr, -dq)))
+    for dq in (-1, 1):
+        send(0, 0, dq, WIDE.index((0, -dq)))
+    pool_recv[WIDE.index((0, 0))] = tile
+
+    for k, (dr, dq) in enumerate(NEAR):
+        if dr < 0:
+            near[k].wait_recv()
+    below = side_columns(2)
+    for v in range(4):
+        ext[v, OWN + HB : OWN + HB + 2, 0:WB] = jnp.where(row_ok(1), row_recv[1, 2 * v : 2 * v + 2, :], 0.0)
+        ext[v, OWN + HB : OWN + HB + 2, WB:WE] = below[HB * v : HB * v + 2]
+    make_taps(40, 8)
+    last_row = fine_row(HB - 1, window(432, slice(0, WB)))
+    outer_row = fine_row(HB, window(480, slice(0, WB)), row_ok(1))
+    pool_send[1] = sums_of(middle + last_row, outer_row)
+    tile = sums_of(middle + first_row + last_row, outer_row)
+    pool_send[2] = tile
+    for dr in (-1, -2):
+        for dq in (-1, 0, 1):
+            send(1, dr, dq, WIDE.index((-dr, -dq)))
+    for dq in (-1, 1):
+        send(2, 0, dq, 16 - dq)
+    pool_recv[16] = tile
 
     side_lane = lax.broadcasted_iota(jnp.int32, (64, 128), 1)
     right_gate = jnp.where(col_ok(1), 1.0, 0.0)
@@ -251,8 +291,6 @@
     lax.fori_loop(0, 4, side_rows, 0, unroll=True)
     for at, r, e, gate in ((48, 3, 0, row_ok(-1)), (480, 0, 33, row_ok(1))):
         gate = jnp.where(gate, 1.0, 0.0)
-        value = gated(dot(a1[r], window(at, slice(0, WB)))) * gate
-        fine[e * 64 : e * 64 + 64, 0:WB] = value.astype(BF16)
         value = gated(dot(a1[r], window(at, slice(WB, WE)))) * side_gate * gate
         fine[e * 64 : e * 64 + 64, WB:WE] = value.astype(BF16)
 
@@ -283,9 +321,20 @@
 
     for copy in wide:
         copy.wait()
+    for copy in near:
+        copy.wait_send()
     cells = []
-    for k, (dr, dq) in enumerate(WIDE):
-        cells.append(jnp.where(jnp.logical_and(row_ok(dr), col_ok(dq)), pool_recv[k], 0.0))
+    for dr, dq in WIDE:
+        if dr == 0:
+            cell = pool_recv[16 + dq]
+        else:
+            step = 1 if dr > 0 else -1
+            if dr == 1:
+                other = pool_recv[16 + dq]
+            else:
+                other = pool_recv[WIDE.index((dr - step, dq))]
+            cell = pool_recv[WIDE.index((dr, dq))] + pltpu.roll(other, 64, 1)
+        cells.append(jnp.where(jnp.logical_and(row_ok(dr), col_ok(dq)), cell, 0.0))
     cells = jnp.concatenate(cells, axis=0).astype(BF16)
     entering = dot(cells[:, 0:64], wd_v[...])
     coarse[0:8] = jnp.zeros((8, 256), F32)
@@ -367,8 +416,8 @@
                 vmem((2, 8, 128), F32),
                 vmem((2, 8, WB), F32),
                 vmem((2, 3, 8, 128), F32),
-                vmem((8, 128), F32),
-                vmem((15, 8, 128), F32),
+                vmem((3, 8, 128), F32),
+                vmem((18, 8, 128), F32),
                 vmem((4, 48, WE), F32),
                 vmem((3, 576, 128), F32),
                 vmem((576, WE), BF16),
@@ -394,8 +443,8 @@
                 pltpu.SemaphoreType.DMA,
                 pltpu.SemaphoreType.DMA((8,)),
                 pltpu.SemaphoreType.DMA((8,)),
-                pltpu.SemaphoreType.DMA((15,)),
-                pltpu.SemaphoreType.DMA((15,)),
+                pltpu.SemaphoreType.DMA((16,)),
+                pltpu.SemaphoreType.DMA((18,)),
             ],
             compiler_params=pltpu.CompilerParams(
                 collective_id=0, has_side_effects=True, vmem_limit_bytes=67043328

time: 28.1 us -> 25.5 us (0.907)
  the two profiles are of different devices: /device:TPU:32 before, /device:TPU:1 now
where the time goes in v3:
time: 25.5 us; the launch traced here: 25.4 us
  Pallas kernels  23.9 us (94%)
  local copies, waits for them, and re-layouts  1.57 us (6%)
    pallas_call x1, Pallas kernels, on_device(): pl.pallas_call(functools.partial(kernel, n_rows, n_cols, n_ty), out_shape...  23.9 us
    unnamed x1, local copies, waits for them, and re-layouts  1.57 us

profile of v3, /device:TPU:1, one launch (start us, length us, event | category | flops | bytes accessed | tf_op | source)
XLA Modules:
  0.0 25.4 jit_solution(1711801447658652616)
XLA Ops:
  0.0 23.9 %shard_map.109 = f32[4,32,256]{2,1,0:T(8,128)} custom-call(f32[4,32,256]{2,1,0:T(8,128)} %noisy_h.1, f32[4,64]{1,0:T(4,128)} %bitcast.4, bf16[3,3,64,64]{3,2,1,0:T(8,128)(2,1)} %kf_h.1, bf16[64,256]{1,0:T(8,128)(2,1)} %bitcast.3, bf16[3,3,256,256]{3,2,1,0:T(8,128)(2,1)} %kc_h.1, bf16[64,256]{1,0:T(8,128)(2,1)} %wu_h.1, bf16[3,3,64,64]{3,2,1,0:T(8,128)(2,1)} %kl_h.1, ...), custom_call_target="tpu_custom_call" | custom-call | tf_op jit(solution)/shard_map/pallas_call | solution.py:408
  23.9 1.6 %copy.13 = f32[4,32,256]{2,1,0:T(8,128)} copy(f32[4,32,256]{2,1,0:T(8,128)} %shard_map.109) | data formatting | bytes 262144

commit v4 on v3

--- a/solution.py
+++ b/solution.py
@@ -47,8 +47,8 @@
     noisy_v, w_in_v, kf_v, wd_v, kc_v, wu_v, kl_v, wo_v, cell_v, count_v, obs_v,
     row_send, col_send, row_recv, col_recv, pool_send, pool_recv,
     ext, taps, taps_h, taps_l, a1, a2, w9, wo8, expand, fine, fine_l, fine_r, acc,
-    station_a, station_b, fine_three, coarse, up_b, s_ref, raised_ref, out_v,
-    in_sem, out_sem, near_send, near_recv, wide_send, wide_recv,
+    station_a, station_b, fine_three, coarse, up_b, s_ref, raised_ref,
+    in_sem, near_send, near_recv, wide_send, wide_recv,
 ):
     row = lax.axis_index("grp") * n_ty + lax.axis_index("ty")
     col = lax.axis_index("tx")
@@ -72,10 +72,19 @@
     for load in loads:
         load.start()
 
+    def there(dr, dq):
+        if dq == 0:
+            return row_ok(dr)
+        return col_ok(dq) if dr == 0 else jnp.logical_and(row_ok(dr), col_ok(dq))
+
     barrier = pltpu.get_barrier_semaphore()
     for dr, dq in WIDE:
         if (dr, dq) != (0, 0):
-            pl.semaphore_signal(barrier, inc=1, device_id=device(dr, dq), device_id_type=MESH)
+
+            @pl.when(there(dr, dq))
+            def _(dr=dr, dq=dq):
+                pl.semaphore_signal(barrier, inc=1, device_id=device(dr, dq), device_id_type=MESH)
+
 
     loads[0].wait()
     for v in range(4):
@@ -86,7 +95,10 @@
     col_send[0] = first.T[0:8, :]
     col_send[1] = last.T[120:128, :]
 
-    pl.semaphore_wait(barrier, len(WIDE) - 1)
+    above_count = jnp.minimum(row, 2)
+    below_count = jnp.minimum(n_rows - 1 - row, 2)
+    sides = jnp.minimum(col, 1) + jnp.minimum(n_cols - 1 - col, 1)
+    pl.semaphore_wait(barrier, (above_count + below_count + 1) * (sides + 1) - 1)
     near = []
     for k, (dr, dq) in enumerate(NEAR):
         if dq == 0:
@@ -102,8 +114,8 @@
                 device_id=device(dr, dq), device_id_type=MESH,
             )
         )
-    for copy in near:
-        copy.start()
+    for copy, (dr, dq) in zip(near, NEAR):
+        pl.when(there(dr, dq))(copy.start)
 
     for load in loads[1:]:
         load.wait()
@@ -157,7 +169,7 @@
 
     for k, (dr, dq) in enumerate(NEAR):
         if dr >= 0:
-            near[k].wait_recv()
+            pl.when(there(-dr, -dq))(near[k].wait_recv)
     ext[...] = jnp.zeros_like(ext)
 
     def side_columns(k):
@@ -230,7 +242,7 @@
     outer_row = fine_row(-1, window(48, slice(0, WB)), row_ok(-1))
     tile = sums_of(middle + first_row, outer_row)
     pool_send[0] = tile
-    wide = []
+    wide, wide_at = [], []
 
     def send(which, dr, dq, slot):
         wide.append(
@@ -239,7 +251,8 @@
                 recv_sem=wide_recv.at[slot], device_id=device(dr, dq), device_id_type=MESH,
             )
         )
-        wide[-1].start()
+        pl.when(there(dr, dq))(wide[-1].start)
+        wide_at.append((dr, dq))
 
     for dr in (1, 2):
         for dq in (-1, 0, 1):
@@ -250,7 +263,7 @@
 
     for k, (dr, dq) in enumerate(NEAR):
         if dr < 0:
-            near[k].wait_recv()
+            pl.when(there(-dr, -dq))(near[k].wait_recv)
     below = side_columns(2)
     for v in range(4):
         ext[v, OWN + HB : OWN + HB + 2, 0:WB] = jnp.where(row_ok(1), row_recv[1, 2 * v : 2 * v + 2, :], 0.0)
@@ -319,10 +332,10 @@
 
     lax.fori_loop(0, 16, last_rows, 0, unroll=True)
 
-    for copy in wide:
-        copy.wait()
-    for copy in near:
-        copy.wait_send()
+    for copy, (dr, dq) in zip(wide, wide_at):
+        pl.when(there(-dr, -dq))(copy.wait_recv)
+    for copy, (dr, dq) in zip(wide + near, wide_at + list(NEAR)):
+        pl.when(there(dr, dq))(copy.wait_send)
     cells = []
     for dr, dq in WIDE:
         if dr == 0:
@@ -380,10 +393,7 @@
         denoised = dot(wo8[...], fine_three[512 * g : 512 * g + 512, :])
         for v in range(4):
             rows = slice(8 * g, 8 * g + 8)
-            out_v[v, rows, :] = station_a[v, rows, :] + station_b[rows, :] * denoised[8 * v : 8 * v + 8]
-    store = pltpu.make_async_copy(out_v, out_h, out_sem)
-    store.start()
-    store.wait()
+            out_h[v, rows, :] = station_a[v, rows, :] + station_b[rows, :] * denoised[8 * v : 8 * v + 8]
 
 
 def dot_hi(w_in):
@@ -405,11 +415,12 @@
         count = count.reshape(1, 1, 128)
         args = (noisy, w_in, kf, wd, kc, wu, kl, wo, cell, count, obs)
         vmem = pltpu.VMEM
+        args = tuple(pltpu.with_memory_space_constraint(x, pltpu.HBM) for x in args)
         return pl.pallas_call(
             functools.partial(kernel, n_rows, n_cols, n_ty),
             out_shape=jax.ShapeDtypeStruct(noisy.shape, noisy.dtype),
             in_specs=[pl.BlockSpec(memory_space=pltpu.HBM)] * 11,
-            out_specs=pl.BlockSpec(memory_space=pl.ANY),
+            out_specs=pl.BlockSpec(memory_space=pltpu.VMEM),
             scratch_shapes=[vmem(x.shape, x.dtype) for x in args]
             + [
                 vmem((2, 8, WB), F32),
@@ -438,16 +449,14 @@
                 vmem((9, 64, WB), BF16),
                 vmem((3, 64, WB), F32),
                 vmem((64, WB), F32),
-                vmem((4, HB, WB), F32),
                 pltpu.SemaphoreType.DMA((11,)),
-                pltpu.SemaphoreType.DMA,
                 pltpu.SemaphoreType.DMA((8,)),
                 pltpu.SemaphoreType.DMA((8,)),
                 pltpu.SemaphoreType.DMA((16,)),
                 pltpu.SemaphoreType.DMA((18,)),
             ],
             compiler_params=pltpu.CompilerParams(
-                collective_id=0, has_side_effects=True, vmem_limit_bytes=67043328
+                collective_id=0, has_side_effects=True, vmem_limit_bytes=50*1024*1024
             ),
         )(*args)
 

time: 25.5 us -> 21.2 us (0.83)
  the two profiles are of different devices: /device:TPU:1 before, /device:TPU:32 now
where the time goes in v4:
time: 21.2 us; the launch traced here: 21.1 us
  Pallas kernels  20.5 us (97%)
  local copies, waits for them, and re-layouts  0.66 us (3%)
    pallas_call x1, Pallas kernels, on_device(): pl.pallas_call(functools.partial(kernel, n_rows, n_cols, n_ty), out_shape...  20.5 us
    unnamed x1, local copies, waits for them, and re-layouts  0.66 us

profile of v4, /device:TPU:32, one launch (start us, length us, event | category | flops | bytes accessed | tf_op | source)
XLA Modules:
  0.0 21.1 jit_solution(7508955058338733428)
XLA Ops:
  0.0 20.5 %shard_map.109 = f32[4,32,256]{2,1,0:T(8,128)S(1)} custom-call(f32[4,32,256]{2,1,0:T(8,128)} %noisy_h.1, f32[4,64]{1,0:T(4,128)} %bitcast.4, bf16[3,3,64,64]{3,2,1,0:T(8,128)(2,1)} %kf_h.1, bf16[64,256]{1,0:T(8,128)(2,1)} %bitcast.3, bf16[3,3,256,256]{3,2,1,0:T(8,128)(2,1)} %kc_h.1, bf16[64,256]{1,0:T(8,128)(2,1)} %wu_h.1, bf16[3,3,64,64]{3,2,1,0:T(8,128)(2,1)} %kl_h.1, ...), custom_call_target="tpu_custom_call" | custom-call | tf_op jit(solution)/shard_map/pallas_call | solution.py:419
  20.5 0.7 %copy.13 = f32[4,32,256]{2,1,0:T(8,128)} copy(f32[4,32,256]{2,1,0:T(8,128)S(1)} %shard_map.109) | data formatting | bytes 262144

commit v5 on v4

--- a/solution.py
+++ b/solution.py
@@ -46,7 +46,7 @@
     out_h,
     noisy_v, w_in_v, kf_v, wd_v, kc_v, wu_v, kl_v, wo_v, cell_v, count_v, obs_v,
     row_send, col_send, row_recv, col_recv, pool_send, pool_recv,
-    ext, taps, taps_h, taps_l, a1, a2, w9, wo8, expand, fine, fine_l, fine_r, acc,
+    ext, taps, taps_h, taps_l, a1, a2, w9, wo8, expand, fine, fine_l, fine_r, acc, edge_ref,
     station_a, station_b, fine_three, coarse, up_b, s_ref, raised_ref,
     in_sem, near_send, near_recv, wide_send, wide_recv,
 ):
@@ -167,48 +167,51 @@
         station_a[v] = 0.5 * noisy_v[v] + 0.25 * sums[HB * v : HB * (v + 1)]
     station_b[...] = 0.5 - 0.25 * sums[HB * 4 :]
 
-    for k, (dr, dq) in enumerate(NEAR):
-        if dr >= 0:
-            pl.when(there(-dr, -dq))(near[k].wait_recv)
     ext[...] = jnp.zeros_like(ext)
+    for v in range(4):
+        ext[v, OWN : OWN + HB, 0:WB] = noisy_v[v]
+
+    def make_taps(start, size):
+        rows = slice(12 * start, 12 * (start + size))
+        for v in range(4):
+            left, right = ext[v, start : start + size, 0:128], ext[v, start : start + size, 128:256]
+            spot = lax.broadcasted_iota(jnp.int32, left.shape, 1)
+            up = [pltpu.roll(x, 1, 1) for x in (left, right)]
+            down = [pltpu.roll(x, 127, 1) for x in (left, right)]
+            shifted = (
+                (jnp.where(spot < 1, 0.0, up[0]), left, jnp.where(spot < 127, down[0], down[1])),
+                (jnp.where(spot < 1, up[0], up[1]), right, jnp.where(spot < 127, down[1], 0.0)),
+            )
+            for t in range(2):
+                for q in range(3):
+                    taps[t, pl.ds(12 * start + 4 * q + v, size, stride=12), :] = shifted[t][q]
+        for t in range(2):
+            high, low = split2(taps[t, rows])
+            taps_h[rows, 128 * t : 128 * t + 128] = high
+            taps_l[rows, 128 * t : 128 * t + 128] = low
+
+    def make_side_taps(start, size):
+        for v in range(4):
+            rows = slice(start, start + size)
+            spot = lax.broadcasted_iota(jnp.int32, (size, 128), 1)
+            near_columns = jnp.where(
+                spot < 4, pltpu.roll(ext[v, rows, 0:128], 2, 1), pltpu.roll(ext[v, rows, 128:256], 6, 1)
+            )
+            inside = jnp.logical_and(spot >= 2, spot < 6)
+            here = jnp.where(inside, near_columns, ext[v, rows, WB:WE])
+            for q, value in enumerate((pltpu.roll(here, 1, 1), here, pltpu.roll(here, 127, 1))):
+                taps[2, pl.ds(12 * start + 4 * q + v, size, stride=12), :] = value
 
     def side_columns(k):
         right = jnp.where(jnp.logical_and(row_ok(k - 1), col_ok(1)), col_recv[1, k], 0.0)
         left = jnp.where(jnp.logical_and(row_ok(k - 1), col_ok(-1)), col_recv[0, k], 0.0)
-        return jnp.concatenate([right, jnp.zeros((112, 128), F32), left], axis=0).T
-
-    above, beside = side_columns(0), side_columns(1)
-    for v in range(4):
-        ext[v, OWN : OWN + HB, 0:WB] = noisy_v[v]
-        ext[v, OWN - 2 : OWN, 0:WB] = jnp.where(row_ok(-1), row_recv[0, 2 * v : 2 * v + 2, :], 0.0)
-        ext[v, OWN - 2 : OWN, WB:WE] = above[HB * v + HB - 2 : HB * v + HB]
-        ext[v, OWN : OWN + HB, WB:WE] = beside[HB * v : HB * (v + 1)]
-
-    def make_taps(start, size):
-        for v in range(4):
-            for t in range(3):
-                here, before, after = (
-                    ext[v, start : start + size, 128 * ((t + d) % 3) : 128 * ((t + d) % 3) + 128] for d in (0, 2, 1)
-                )
-                spot = lax.broadcasted_iota(jnp.int32, here.shape, 1)
-                shifted = (
-                    jnp.where(spot < 1, pltpu.roll(before, 1, 1), pltpu.roll(here, 1, 1)),
-                    here,
-                    jnp.where(spot < 127, pltpu.roll(here, 127, 1), pltpu.roll(after, 127, 1)),
-                )
-                for q in range(3):
-                    taps[t, pl.ds(12 * start + 4 * q + v, size, stride=12), :] = shifted[q]
-        rows = slice(12 * start, 12 * (start + size))
-        for t in range(3):
-            high, low = split2(taps[t, rows])
-            taps_h[rows, 128 * t : 128 * t + 128] = high
-            taps_l[rows, 128 * t : 128 * t + 128] = low
-
-    make_taps(0, 48)
-
-    def window(at, lanes):
-        high = taps_h[pl.ds(at, 80), lanes]
-        return jnp.concatenate([high, taps_l[pl.ds(at, 80), lanes], high], axis=0)
+        place = lax.broadcasted_iota(jnp.int32, (8, 128), 0)
+        both = jnp.where(place < 2, pltpu.roll(left, 2, 0), jnp.where(place >= 6, pltpu.roll(right, 6, 0), 0.0))
+        return jnp.concatenate([both, jnp.zeros((120, 128), F32)], axis=0).T
+
+    def window(at):
+        high = taps_h[pl.ds(at, 80), :]
+        return jnp.concatenate([high, taps_l[pl.ds(at, 80), :], high], axis=0)
 
     def gated(both):
         h = both[0:64]
@@ -221,26 +224,63 @@
         fine[64 * (i + 1) : 64 * (i + 2), 0:WB] = value.astype(BF16)
         return value
 
-    into = lax.broadcasted_iota(jnp.int32, (8, WB), 1) // 32 == lax.broadcasted_iota(jnp.int32, (8, WB), 0)
-    into = into.astype(F32).astype(BF16)
-
-    def sums_of(upper, lower):
-        high, low = split2(jnp.concatenate([upper, lower], axis=0))
-        return (dot_t(into, high) + dot_t(into, low)) * (1.0 / 1024.0)
-
+    make_taps(0, 48)
     middle = jnp.zeros((64, WB), F32)
     for g in range(8):
-        rhs = window(96 + 48 * g, slice(0, WB))
+        rhs = window(96 + 48 * g)
         for r in range(4):
-            i = 4 * g + r
-            if i < HB - 1:
-                value = fine_row(i, rhs)
-                if i == 0:
-                    first_row = value
-                else:
-                    middle = middle + value
-    outer_row = fine_row(-1, window(48, slice(0, WB)), row_ok(-1))
-    tile = sums_of(middle + first_row, outer_row)
+            if 0 < 4 * g + r < HB - 1:
+                middle = middle + fine_row(4 * g + r, rhs)
+
+    lane = lax.broadcasted_iota(jnp.int32, (64, 128), 1)
+    group, spot = lane // 8, lane % 8
+    gate = jnp.where(spot == 1, jnp.where(col_ok(-1), 1.0, 0.0), jnp.where(spot == 6, jnp.where(col_ok(1), 1.0, 0.0), 1.0))
+    gate = gate * jnp.where(group == 8, jnp.where(row_ok(-1), 1.0, 0.0), jnp.where(group == 9, jnp.where(row_ok(1), 1.0, 0.0), 1.0))
+    starts = [96 + 48 * g for g in range(8)] + [48, 480]
+    tap_lane = lax.broadcasted_iota(jnp.int32, (80, 128), 1) // 8
+
+    def side_inputs(groups, packed):
+        for g in groups:
+            value = taps[2, pl.ds(starts[g], 80), :]
+            packed = jnp.where(tap_lane == g, value if g == 0 else pltpu.roll(value, 8 * g, 1), packed)
+        high, low = split2(packed)
+        return packed, jnp.concatenate([high, low, high], axis=0)
+
+    def side_rows(r, rhs):
+        value = gated(dot(a1[r], rhs)) * gate
+        edge_ref[r] = value
+        return value
+
+    pixel = lax.broadcasted_iota(jnp.int32, (8, WE), 1)
+    cell_of = jnp.where(pixel < WB, pixel // 32, jnp.where(pixel % 8 == 2, 0, jnp.where(pixel % 8 == 5, 7, 8)))
+    cell_of = jnp.where(jnp.logical_or(pixel == 0, pixel == WB - 1), 8, cell_of)
+    into = (cell_of == lax.broadcasted_iota(jnp.int32, (8, WE), 0)).astype(F32).astype(BF16)
+
+    def sums_of(upper, upper_side, lower, lower_side):
+        stack = jnp.concatenate(
+            [jnp.concatenate([upper, upper_side], axis=1), jnp.concatenate([lower, lower_side], axis=1)], axis=0
+        )
+        high, low = split2(stack)
+        return (dot_t(into, high) + dot_t(into, low)) * (1.0 / 1024.0)
+
+    for k, (dr, dq) in enumerate(NEAR):
+        if dr >= 0:
+            pl.when(there(-dr, -dq))(near[k].wait_recv)
+    above, beside = side_columns(0), side_columns(1)
+    for v in range(4):
+        ext[v, OWN - 2 : OWN, 0:WB] = jnp.where(row_ok(-1), row_recv[0, 2 * v : 2 * v + 2, :], 0.0)
+        ext[v, OWN - 2 : OWN, WB:WE] = above[HB * v + HB - 2 : HB * v + HB]
+        ext[v, OWN : OWN + HB, WB:WE] = beside[HB * v : HB * (v + 1)]
+    make_taps(0, 16)
+    make_side_taps(0, 48)
+    first_row = fine_row(0, window(96))
+    outer_row = fine_row(-1, window(48), row_ok(-1))
+    packed, rhs = side_inputs(range(10), jnp.zeros((80, 128), F32))
+    side = [side_rows(r, rhs) for r in range(4)]
+    inner_side = jnp.where(lane < 64, side[1] + side[2], 0.0)
+    side_sum = inner_side + jnp.where(lane < 64, side[0], 0.0) + jnp.where(lane < 56, side[3], 0.0)
+    outer_side = jnp.where(group == 8, side[3], 0.0)
+    tile = sums_of(middle + first_row, side_sum, outer_row, outer_side)
     pool_send[0] = tile
     wide, wide_at = [], []
 
@@ -269,10 +309,17 @@
         ext[v, OWN + HB : OWN + HB + 2, 0:WB] = jnp.where(row_ok(1), row_recv[1, 2 * v : 2 * v + 2, :], 0.0)
         ext[v, OWN + HB : OWN + HB + 2, WB:WE] = below[HB * v : HB * v + 2]
     make_taps(40, 8)
-    last_row = fine_row(HB - 1, window(432, slice(0, WB)))
-    outer_row = fine_row(HB, window(480, slice(0, WB)), row_ok(1))
-    pool_send[1] = sums_of(middle + last_row, outer_row)
-    tile = sums_of(middle + first_row + last_row, outer_row)
+    make_side_taps(40, 8)
+    last_row = fine_row(HB - 1, window(432))
+    outer_row = fine_row(HB, window(480), row_ok(1))
+    packed, rhs = side_inputs((7, 9), packed)
+    low_side, top_side = side_rows(3, rhs), side_rows(0, rhs)
+    outer_side = jnp.where(group == 9, top_side, 0.0)
+    inner_side = inner_side + jnp.where(lane < 64, low_side, 0.0)
+    all_side = inner_side + jnp.where(lane < 64, top_side, 0.0)
+    low_sum = inner_side + jnp.where(jnp.logical_and(lane >= 8, lane < 64), top_side, 0.0)
+    pool_send[1] = sums_of(middle + last_row, low_sum, outer_row, outer_side)
+    tile = sums_of(middle + first_row + last_row, all_side, outer_row, outer_side)
     pool_send[2] = tile
     for dr in (-1, -2):
         for dq in (-1, 0, 1):
@@ -281,46 +328,20 @@
         send(2, 0, dq, 16 - dq)
     pool_recv[16] = tile
 
-    side_lane = lax.broadcasted_iota(jnp.int32, (64, 128), 1)
-    right_gate = jnp.where(col_ok(1), 1.0, 0.0)
-    left_gate = jnp.where(col_ok(-1), 1.0, 0.0)
-    side_gate = jnp.where(side_lane < 64, right_gate, left_gate)
-
-    def side_rows(g, carry):
-        rhs = jnp.concatenate(
-            [
-                window(pl.multiple_of(96 + 96 * g, 16), slice(WB, WE)),
-                window(pl.multiple_of(144 + 96 * g, 16), slice(WB, WE)),
-            ],
-            axis=1,
-        )
-        for r in range(4):
-            value = gated(dot(a1[r], rhs))
-            for k in range(2):
-                at = pl.multiple_of((8 * g + 4 * k + r + 1) * 64, 64)
-                fine[pl.ds(at, 64), WB:WE] = (value[:, 128 * k : 128 * k + 128] * side_gate).astype(BF16)
-        return carry
-
-    lax.fori_loop(0, 4, side_rows, 0, unroll=True)
-    for at, r, e, gate in ((48, 3, 0, row_ok(-1)), (480, 0, 33, row_ok(1))):
-        gate = jnp.where(gate, 1.0, 0.0)
-        value = gated(dot(a1[r], window(at, slice(WB, WE)))) * side_gate * gate
-        fine[e * 64 : e * 64 + 64, WB:WE] = value.astype(BF16)
-
-    def shift_rows(e, carry):
-        at = pl.multiple_of(e * 64, 64)
-        tile = [fine[pl.ds(at, 64), 128 * t : 128 * t + 128] for t in range(3)]
-        spot = lax.broadcasted_iota(jnp.int32, (64, 128), 1)
-        tile = [x.astype(F32) for x in tile]
-        up = [pltpu.roll(x, 1, 1) for x in tile]
-        down = [pltpu.roll(x, 127, 1) for x in tile]
-        fine_l[pl.ds(at, 64), 0:128] = jnp.where(spot < 1, up[2], up[0]).astype(BF16)
-        fine_l[pl.ds(at, 64), 128:256] = jnp.where(spot < 1, up[0], up[1]).astype(BF16)
-        fine_r[pl.ds(at, 64), 0:128] = jnp.where(spot < 127, down[0], down[1]).astype(BF16)
-        fine_r[pl.ds(at, 64), 128:256] = jnp.where(spot < 127, down[1], down[2]).astype(BF16)
-        return carry
-
-    lax.fori_loop(0, HB + 2, shift_rows, 0, unroll=True)
+    for e in range(HB + 2):
+        g = 8 if e == 0 else 9 if e == HB + 1 else (e - 1) // 4
+        edge = edge_ref[(e - 1) % 4]
+        rows = slice(64 * e, 64 * e + 64)
+        left, right = fine[rows, 0:128].astype(F32), fine[rows, 128:256].astype(F32)
+        up = [pltpu.roll(x, 1, 1) for x in (left, right)]
+        down = [pltpu.roll(x, 127, 1) for x in (left, right)]
+        turned = [pltpu.roll(edge, (at - 8 * g) % 128, 1) for at in (-1, -2, 122, 121)]
+        fine_l[rows, 0:128] = jnp.where(lane < 2, turned[0], up[0]).astype(BF16)
+        fine_l[rows, 128:256] = jnp.where(lane < 1, up[0], up[1]).astype(BF16)
+        fine_r[rows, 0:128] = jnp.where(lane < 127, down[0], down[1]).astype(BF16)
+        fine_r[rows, 128:256] = jnp.where(lane < 126, down[1], turned[3]).astype(BF16)
+        fine[rows, 0:128] = jnp.where(lane < 1, turned[1], left).astype(BF16)
+        fine[rows, 128:256] = jnp.where(lane < 127, right, turned[2]).astype(BF16)
 
     def last_rows(k, carry):
         at = pl.multiple_of(k * 128, 128)
@@ -431,17 +452,18 @@
                 vmem((18, 8, 128), F32),
                 vmem((4, 48, WE), F32),
                 vmem((3, 576, 128), F32),
-                vmem((576, WE), BF16),
-                vmem((576, WE), BF16),
+                vmem((576, WB), BF16),
+                vmem((576, WB), BF16),
                 vmem((4, 128, 240), BF16),
                 vmem((3, 128, 256), BF16),
                 vmem((64, 576), BF16),
                 vmem((32, 512), BF16),
                 vmem((9, 72, WB), BF16),
-                vmem((34 * 64, WE), BF16),
+                vmem((34 * 64, WB), BF16),
                 vmem((34 * 64, WB), BF16),
                 vmem((34 * 64, WB), BF16),
                 vmem((HB * 64, WB), F32),
+                vmem((4, 64, 128), F32),
                 vmem((4, HB, WB), F32),
                 vmem((HB, WB), F32),
                 vmem((HB * 64, WB), BF16),

time: 21.2 us -> 21 us (level)
  Pallas kernels: 20.5 us -> 20.2 us
    pallas_call x1, Pallas kernels: 20.5 us -> 20.2 us  [on_device(): pl.pallas_call(functools.partial(kernel, n_rows, n_cols, n_ty), out_shape...]
where the time goes in v5:
time: 21 us; the launch traced here: 20.9 us
  Pallas kernels  20.2 us (96%)
  local copies, waits for them, and re-layouts  0.66 us (3%)
    pallas_call x1, Pallas kernels, on_device(): pl.pallas_call(functools.partial(kernel, n_rows, n_cols, n_ty), out_shape...  20.2 us
    unnamed x1, local copies, waits for them, and re-layouts  0.66 us

profile of v5, /device:TPU:32, one launch (start us, length us, event | category | flops | bytes accessed | tf_op | source)
XLA Modules:
  0.0 20.9 jit_solution(16857749859019437207)
XLA Ops:
  0.0 20.2 %shard_map.109 = f32[4,32,256]{2,1,0:T(8,128)S(1)} custom-call(f32[4,32,256]{2,1,0:T(8,128)} %noisy_h.1, f32[4,64]{1,0:T(4,128)} %bitcast.4, bf16[3,3,64,64]{3,2,1,0:T(8,128)(2,1)} %kf_h.1, bf16[64,256]{1,0:T(8,128)(2,1)} %bitcast.3, bf16[3,3,256,256]{3,2,1,0:T(8,128)(2,1)} %kc_h.1, bf16[64,256]{1,0:T(8,128)(2,1)} %wu_h.1, bf16[3,3,64,64]{3,2,1,0:T(8,128)(2,1)} %kl_h.1, ...), custom_call_target="tpu_custom_call" | custom-call | tf_op jit(solution)/shard_map/pallas_call | solution.py:440
  20.2 0.7 %copy.13 = f32[4,32,256]{2,1,0:T(8,128)} copy(f32[4,32,256]{2,1,0:T(8,128)S(1)} %shard_map.109) | data formatting | bytes 262144

commit v6 on v5

--- a/solution.py
+++ b/solution.py
@@ -46,17 +46,17 @@
     out_h,
     noisy_v, w_in_v, kf_v, wd_v, kc_v, wu_v, kl_v, wo_v, cell_v, count_v, obs_v,
     row_send, col_send, row_recv, col_recv, pool_send, pool_recv,
-    ext, taps, taps_h, taps_l, a1, a2, w9, wo8, expand, fine, fine_l, fine_r, acc, edge_ref,
-    station_a, station_b, fine_three, coarse, up_b, s_ref, raised_ref,
+    ext, taps, taps_h, taps_l, a1, a2, enter_w, leave_w, wo8, expand, fine, fine_l, fine_r, acc, edge_ref,
+    station_a, station_b, fine_three, coarse, s_ref, raised_ref,
     in_sem, near_send, near_recv, wide_send, wide_recv,
 ):
     row = lax.axis_index("grp") * n_ty + lax.axis_index("ty")
     col = lax.axis_index("tx")
 
+    row_of = {dr: (lax.div(row + dr, n_ty), lax.rem(row + dr, n_ty)) for dr in range(-2, 3)}
+
     def device(dr, dq):
-        r = lax.rem(row + dr + n_rows, n_rows)
-        q = lax.rem(col + dq + n_cols, n_cols)
-        return (r // n_ty, lax.rem(r, n_ty), q)
+        return row_of[dr] + (col + dq,)
 
     def row_ok(dr):
         return jnp.logical_and(row + dr >= 0, row + dr < n_rows)
@@ -143,18 +143,25 @@
         upper = jnp.concatenate([half[0][q], half[1][q], half[2][q], zero64], axis=1)
         lower = jnp.concatenate([zero64, half[0][q], half[1][q], half[2][q]], axis=1)
         a2[q] = jnp.concatenate([upper, lower], axis=0)
-    w9[...] = jnp.concatenate([half[p][q] for p in range(3) for q in range(3)], axis=1)
+    stack = jnp.concatenate([half[p][q] for p in range(3) for q in range(3)], axis=0)
+    leave_w[0:576] = dot(stack, wu_v[...]).astype(BF16)
+    leave_w[576:640] = wu_v[...]
+    down = jnp.concatenate([wd_v[...], jnp.zeros((64, 256), BF16)], axis=0)
+    for p in range(3):
+        for q in range(3):
+            at = 128 * (3 * p + q)
+            enter_w[at : at + 128] = dot_t(down, kc_v[p, q]).astype(BF16)
     pick = (lax.broadcasted_iota(jnp.int32, (32, 4), 0) // 8 == lax.broadcasted_iota(jnp.int32, (32, 4), 1))
     spread = dot(pick.astype(BF16), wo_v[...])
     spread = jnp.concatenate([spread] * 8, axis=1)
     same = lax.broadcasted_iota(jnp.int32, (32, 512), 0) % 8 == lax.broadcasted_iota(jnp.int32, (32, 512), 1) // 64
     wo8[...] = jnp.where(same, spread, 0.0).astype(BF16)
-    cells = lax.broadcasted_iota(jnp.int32, (72, WB), 0)
-    pixel = lax.broadcasted_iota(jnp.int32, (72, WB), 1)
-    for rho in range(3):
-        for q in range(3):
-            want = rho * 24 + 7 + (pixel + (32 + q - 1)) // 32
-            expand[rho * 3 + q] = (cells == want).astype(F32).astype(BF16)
+    place = lax.broadcasted_iota(jnp.int32, (128, WB), 0)
+    pixel = lax.broadcasted_iota(jnp.int32, (128, WB), 1)
+    for q in range(3):
+        want = 7 + (pixel + (32 + q - 1)) // 32
+        found = jnp.logical_and(place < 72, place % 24 == want)
+        expand[128 * q : 128 * q + 128] = found.astype(F32).astype(BF16)
 
     cell = cell_v[0]
     count = count_v[0].astype(F32)
@@ -369,32 +376,45 @@
                 other = pool_recv[WIDE.index((dr - step, dq))]
             cell = pool_recv[WIDE.index((dr, dq))] + pltpu.roll(other, 64, 1)
         cells.append(jnp.where(jnp.logical_and(row_ok(dr), col_ok(dq)), cell, 0.0))
-    cells = jnp.concatenate(cells, axis=0).astype(BF16)
-    entering = dot(cells[:, 0:64], wd_v[...])
-    coarse[0:8] = jnp.zeros((8, 256), F32)
-    coarse[128:136] = jnp.zeros((8, 256), F32)
-    coarse[8:128] = entering.astype(BF16).astype(F32)
-    total = jnp.zeros((72, 256), F32)
-    for p in range(3):
-        for q in range(3):
-            at = 8 + 24 * p + q - 1
-            total += dot_t(coarse[at : at + 72].astype(BF16), kc_v[p, q])
-    half_total = 0.5 * total
-    leaving = coarse[32:104] + (half_total + half_total * jnp.tanh(half_total))
+    cells = jnp.concatenate(cells, axis=0)
+    coarse[0:8] = jnp.zeros((8, 128), F32)
+    coarse[128:136] = jnp.zeros((8, 128), F32)
+    coarse[8:128] = cells
+    around = jnp.concatenate(
+        [coarse[8 + 24 * p + q - 1 : 80 + 24 * p + q - 1].astype(BF16) for p in range(3) for q in range(3)], axis=1
+    )
+    h = 0.5 * dot(around, enter_w[...])
+    leaving = dot(cells[24:96, 0:64].astype(BF16), wd_v[...]) + (h + h * jnp.tanh(h))
     blocks = []
     for k, (dr, dq) in enumerate(WIDE[3:12]):
         block = leaving[8 * k : 8 * k + 8]
         blocks.append(jnp.where(jnp.logical_and(row_ok(dr), col_ok(dq)), block, 0.0))
-    leaving = jnp.concatenate(blocks, axis=0).astype(BF16)
-    high, low = split2(dot_t(wu_v[...], leaving))
-    for k in range(9):
-        wide_up = dot(high, expand[k])
-        up_b[k] = wide_up.astype(BF16)
-        if k == 4:
-            raised_ref[...] = wide_up + dot(low, expand[k])
-    for edge, rhos in enumerate(((0, 1, 1), (1, 1, 1), (1, 1, 2))):
-        rhs = jnp.concatenate([up_b[rhos[p] * 3 + q] for p in range(3) for q in range(3)], axis=0)
-        s_ref[edge] = dot(w9[...], rhs)
+    leaving = jnp.concatenate(blocks + [jnp.zeros((56, 256), F32)], axis=0).astype(BF16)
+    parts = dot_t(leave_w[...], leaving)
+    cell_lane = lax.broadcasted_iota(jnp.int32, (64, 128), 1)
+    inside = jnp.logical_and(cell_lane >= 24, cell_lane < 48)
+    mixed = []
+    raised = jnp.where(inside, parts[576:640], 0.0)
+    none = jnp.zeros((64, 128), F32)
+    raised_low = raised - raised.astype(BF16).astype(F32)
+    for q in range(3):
+        one, two, three = (parts[64 * (3 * p + q) : 64 * (3 * p + q) + 64] for p in range(3))
+        mixed.append(
+            jnp.concatenate(
+                [
+                    jnp.where(cell_lane < 24, one, jnp.where(inside, two + three, 0.0)),
+                    jnp.where(inside, one + two + three, 0.0),
+                    jnp.where(inside, one + two, jnp.where(cell_lane >= 48, three, 0.0)),
+                    raised if q == 1 else none,
+                    raised_low if q == 1 else none,
+                ],
+                axis=0,
+            ).astype(BF16)
+        )
+    spread = dot(jnp.concatenate(mixed, axis=1), expand[...])
+    for edge in range(3):
+        s_ref[edge] = spread[64 * edge : 64 * edge + 64]
+    raised_ref[...] = spread[192:256] + spread[256:320]
 
     def finish(i, edge):
         at = i * 64 if isinstance(i, int) else pl.multiple_of(i * 64, 64)
@@ -456,9 +476,10 @@
                 vmem((576, WB), BF16),
                 vmem((4, 128, 240), BF16),
                 vmem((3, 128, 256), BF16),
-                vmem((64, 576), BF16),
+                vmem((1152, 256), BF16),
+                vmem((640, 256), BF16),
                 vmem((32, 512), BF16),
-                vmem((9, 72, WB), BF16),
+                vmem((384, WB), BF16),
                 vmem((34 * 64, WB), BF16),
                 vmem((34 * 64, WB), BF16),
                 vmem((34 * 64, WB), BF16),
@@ -467,8 +488,7 @@
                 vmem((4, HB, WB), F32),
                 vmem((HB, WB), F32),
                 vmem((HB * 64, WB), BF16),
-                vmem((136, 256), F32),
-                vmem((9, 64, WB), BF16),
+                vmem((136, 128), F32),
                 vmem((3, 64, WB), F32),
                 vmem((64, WB), F32),
                 pltpu.SemaphoreType.DMA((11,)),

time: 21 us -> 20.4 us (0.971)
  Pallas kernels: 20.2 us -> 19.6 us
    pallas_call x1, Pallas kernels: 20.2 us -> 19.6 us  [on_device(): pl.pallas_call(functools.partial(kernel, n_rows, n_cols, n_ty), out_shape...]
where the time goes in v6:
time: 20.4 us; the launch traced here: 20.3 us
  Pallas kernels  19.6 us (96%)
  local copies, waits for them, and re-layouts  0.66 us (3%)
    pallas_call x1, Pallas kernels, on_device(): pl.pallas_call(functools.partial(kernel, n_rows, n_cols, n_ty), out_shape...  19.6 us
    unnamed x1, local copies, waits for them, and re-layouts  0.66 us

profile of v6, /device:TPU:32, one launch (start us, length us, event | category | flops | bytes accessed | tf_op | source)
XLA Modules:
  0.0 20.3 jit_solution(12942723054342721128)
XLA Ops:
  0.0 19.6 %shard_map.109 = f32[4,32,256]{2,1,0:T(8,128)S(1)} custom-call(f32[4,32,256]{2,1,0:T(8,128)} %noisy_h.1, f32[4,64]{1,0:T(4,128)} %bitcast.4, bf16[3,3,64,64]{3,2,1,0:T(8,128)(2,1)} %kf_h.1, bf16[64,256]{1,0:T(8,128)(2,1)} %bitcast.3, bf16[3,3,256,256]{3,2,1,0:T(8,128)(2,1)} %kc_h.1, bf16[64,256]{1,0:T(8,128)(2,1)} %wu_h.1, bf16[3,3,64,64]{3,2,1,0:T(8,128)(2,1)} %kl_h.1, ...), custom_call_target="tpu_custom_call" | custom-call | tf_op jit(solution)/shard_map/pallas_call | solution.py:460
  19.6 0.7 %copy.13 = f32[4,32,256]{2,1,0:T(8,128)} copy(f32[4,32,256]{2,1,0:T(8,128)S(1)} %shard_map.109) | data formatting | bytes 262144

commit v7 on v6

--- a/solution.py
+++ b/solution.py
@@ -47,7 +47,7 @@
     noisy_v, w_in_v, kf_v, wd_v, kc_v, wu_v, kl_v, wo_v, cell_v, count_v, obs_v,
     row_send, col_send, row_recv, col_recv, pool_send, pool_recv,
     ext, taps, taps_h, taps_l, a1, a2, enter_w, leave_w, wo8, expand, fine, fine_l, fine_r, acc, edge_ref,
-    station_a, station_b, fine_three, coarse, s_ref, raised_ref,
+    station_a, station_b, added, coarse, s_ref, raised_ref,
     in_sem, near_send, near_recv, wide_send, wide_recv,
 ):
     row = lax.axis_index("grp") * n_ty + lax.axis_index("ty")
@@ -69,8 +69,7 @@
         (count_h, count_v), (obs_h, obs_v), (wd_h, wd_v), (wu_h, wu_v), (kc_h, kc_v),
     )
     loads = [pltpu.make_async_copy(src, dst, in_sem.at[k]) for k, (src, dst) in enumerate(pairs)]
-    for load in loads:
-        load.start()
+    loads[0].start()
 
     def there(dr, dq):
         if dq == 0:
@@ -85,6 +84,9 @@
             def _(dr=dr, dq=dq):
                 pl.semaphore_signal(barrier, inc=1, device_id=device(dr, dq), device_id_type=MESH)
 
+
+    for load in loads[1:]:
+        load.start()
 
     loads[0].wait()
     for v in range(4):
@@ -359,11 +361,14 @@
         return carry
 
     lax.fori_loop(0, 16, last_rows, 0, unroll=True)
+    for g in range(4):
+        part = dot(wo8[...], fine[512 * g + 64 : 512 * g + 576, :])
+        for v in range(4):
+            rows = slice(8 * g, 8 * g + 8)
+            station_a[v, rows, :] += station_b[rows, :] * part[8 * v : 8 * v + 8]
 
     for copy, (dr, dq) in zip(wide, wide_at):
         pl.when(there(-dr, -dq))(copy.wait_recv)
-    for copy, (dr, dq) in zip(wide + near, wide_at + list(NEAR)):
-        pl.when(there(dr, dq))(copy.wait_send)
     cells = []
     for dr, dq in WIDE:
         if dr == 0:
@@ -419,9 +424,8 @@
     def finish(i, edge):
         at = i * 64 if isinstance(i, int) else pl.multiple_of(i * 64, 64)
         h = acc[pl.ds(at, 64), :] + s_ref[edge]
-        one = fine[pl.ds(at + 64, 64), 0:WB].astype(F32)
-        value = one + raised_ref[...] + (h + h * jnp.tanh(h))
-        fine_three[pl.ds(at, 64), :] = value.astype(BF16)
+        value = raised_ref[...] + (h + h * jnp.tanh(h))
+        added[pl.ds(at, 64), :] = value.astype(BF16)
 
     def finish_middle(i, carry):
         finish(i, 1)
@@ -431,10 +435,12 @@
     finish(HB - 1, 2)
     lax.fori_loop(1, HB - 1, finish_middle, 0, unroll=True)
     for g in range(4):
-        denoised = dot(wo8[...], fine_three[512 * g : 512 * g + 512, :])
+        denoised = dot(wo8[...], added[512 * g : 512 * g + 512, :])
         for v in range(4):
             rows = slice(8 * g, 8 * g + 8)
             out_h[v, rows, :] = station_a[v, rows, :] + station_b[rows, :] * denoised[8 * v : 8 * v + 8]
+    for copy, (dr, dq) in zip(wide + near, wide_at + list(NEAR)):
+        pl.when(there(dr, dq))(copy.wait_send)
 
 
 def dot_hi(w_in):

time: 20.4 us -> 20.1 us (0.985)
    pallas_call x1, Pallas kernels: 19.6 us -> 19.4 us  [on_device(): pl.pallas_call(functools.partial(kernel, n_rows, n_cols, n_ty), out_shape...]
where the time goes in v7:
time: 20.1 us; the launch traced here: 20 us
  Pallas kernels  19.4 us (97%)
  local copies, waits for them, and re-layouts  0.66 us (3%)
    pallas_call x1, Pallas kernels, on_device(): pl.pallas_call(functools.partial(kernel, n_rows, n_cols, n_ty), out_shape...  19.4 us
    unnamed x1, local copies, waits for them, and re-layouts  0.66 us

profile of v7, /device:TPU:32, one launch (start us, length us, event | category | flops | bytes accessed | tf_op | source)
XLA Modules:
  0.0 20.0 jit_solution(1945357570906686347)
XLA Ops:
  0.0 19.4 %shard_map.109 = f32[4,32,256]{2,1,0:T(8,128)S(1)} custom-call(f32[4,32,256]{2,1,0:T(8,128)} %noisy_h.1, f32[4,64]{1,0:T(4,128)} %bitcast.4, bf16[3,3,64,64]{3,2,1,0:T(8,128)(2,1)} %kf_h.1, bf16[64,256]{1,0:T(8,128)(2,1)} %bitcast.3, bf16[3,3,256,256]{3,2,1,0:T(8,128)(2,1)} %kc_h.1, bf16[64,256]{1,0:T(8,128)(2,1)} %wu_h.1, bf16[3,3,64,64]{3,2,1,0:T(8,128)(2,1)} %kl_h.1, ...), custom_call_target="tpu_custom_call" | custom-call | tf_op jit(solution)/shard_map/pallas_call | solution.py:466
  19.4 0.7 %copy.13 = f32[4,32,256]{2,1,0:T(8,128)} copy(f32[4,32,256]{2,1,0:T(8,128)S(1)} %shard_map.109) | data formatting | bytes 262144
